TPU v7x, 256 devices: a whole 4x4x8 slice. The times are simulated.
256 devices in a mesh: samp: 32 (over x, z), feat: 8 (over y, core).
Axes of the slice: x: 4, y: 4, z: 8, core: 2. Of those that a mesh axis runs over, the one named last changes fastest.
Arguments:
- inputs: bfloat16 [65536, 96], P('samp'), may hold values from -6 to 6
- frequencies: bfloat16 [96, 16384], P(None, 'feat'), may hold values from -0.625 to 0.625
- phases: float32 [16384], P('feat'), may hold values from -3.140625 to 3.140625
- targets: float32 [65536], P('samp'), may hold values from -12 to 12
- block_order: int32 [65536], P('samp'), may hold values from 0 to 2047, as said below
Outputs:
- weights: float32 [16384], P('feat')
- duals: float32 [65536], P('samp')
- objectives: float32 [4, 2], replicated
Inputs may be any that keep to these rules, and one draw needn't show every extreme that they name: `block_order`: within each aligned run of 2048 samples, a permutation of 0 to 2047.
All inputs are finite; a program needn't handle non-finite values.
Results may differ from a plain program's by a relative error of at most 0.0054.
The roundings to bfloat16 on the way count: a program that leaves them out, or rounds other values in their place, can miss the bound.
Values may be sent and summed in bfloat16 or wider, within the bound.
A program may use at most 64 MiB of HBM per device.

v0:
```python
import math

import jax
import jax.numpy as jnp
from jax import lax
from jax.sharding import Mesh
from jax.sharding import PartitionSpec as P

FEATURES = 16384
BLOCK = 256
ROUNDS = 4
SAMP = ("samp_0", "samp_1")


def in_blocks(value, dim, size):
    shape = value.shape
    tiles = value.reshape(*shape[:dim], size, shape[dim] // size, *shape[dim + 1 :])
    return jnp.moveaxis(tiles, dim, 0)


def sum_at_owner(value, axis, dim):
    size = lax.axis_size(axis)
    tiles = lax.all_to_all(in_blocks(value, dim, size), axis, 0, 0, tiled=True)
    return jnp.sum(tiles, axis=0)


def from_everyone(value, axis):
    copies = jnp.broadcast_to(value, (lax.axis_size(axis), *value.shape))
    return lax.all_to_all(copies, axis, split_axis=0, concat_axis=0, tiled=True)


def laid_out(tiles, dim):
    tiles = jnp.moveaxis(tiles, 0, dim)
    shape = tiles.shape
    return tiles.reshape(*shape[:dim], shape[dim] * shape[dim + 1], *shape[dim + 2 :])


def gathered_copies(value, axis, dim):
    tiles = from_everyone(value, axis)
    return laid_out(tiles, dim)


def taken_together(value, axis):
    everything = from_everyone(value, axis)
    return jnp.sum(everything, axis=0)


def packed_total(arrays, axis):
    vector, at, done = (jnp.concatenate([a.reshape(-1) for a in arrays]), 0, [])
    total = taken_together(vector, axis)
    for a in arrays:
        done.append(total[at : at + a.size].reshape(a.shape))
        at += a.size
    return tuple(done)


def by_axis(value, axes):
    for axis in axes:
        value = lax.psum(value, axis)
    return value


def solve_block(factor, vector):
    return jax.scipy.linalg.cho_solve((factor, True), vector)


def on_device(inputs, frequencies, phases, targets, block_order):
    row_count = inputs.shape[0]
    groups = lax.axis_size(SAMP)
    sample_total = row_count * groups
    ridge = 1.0 / BLOCK
    step_scale = BLOCK / sample_total
    block_count = row_count // BLOCK
    feat_count = lax.axis_size("feat")
    own_blocks = block_count // feat_count
    picked = inputs[block_order]
    wanted = targets[block_order]
    angles = jnp.dot(picked, frequencies, preferred_element_type=jnp.float32)
    features = (math.sqrt(2.0 / FEATURES) * jnp.cos(angles + phases)).astype(jnp.bfloat16)
    blocked = features.reshape(block_count, BLOCK, features.shape[1])
    gram_sums = jnp.einsum("bid,bjd->bij", blocked, blocked, preferred_element_type=jnp.float32)
    gram_sums = sum_at_owner(gram_sums, "feat", 0)
    factors = jnp.linalg.cholesky(gram_sums + jnp.eye(BLOCK, dtype=jnp.float32))
    duals = jnp.zeros((row_count,), jnp.float32)
    margins = jnp.zeros((row_count,), jnp.float32)
    weights = jnp.zeros((features.shape[1],), jnp.float32)
    collected = []
    for round_index in range(ROUNDS):
        residual = (wanted - duals - margins).reshape(block_count, BLOCK)
        first = lax.axis_index("feat") * own_blocks
        own_residual = lax.dynamic_slice_in_dim(residual, first, own_blocks, 0)
        own_update = jax.vmap(solve_block)(factors, own_residual)
        update = gathered_copies(own_update, "feat", 0).reshape(row_count)
        duals = duals + update
        update_bf = update.astype(jnp.bfloat16)
        step_term = jnp.dot(update_bf, features, preferred_element_type=jnp.float32) * step_scale
        weights = weights + taken_together(step_term, SAMP)
        weight_bf = weights.astype(jnp.bfloat16)
        norm_part = jnp.sum(weights * weights)
        partial_value = jnp.dot(features, weight_bf, preferred_element_type=jnp.float32)
        margins, norm_feat = packed_total((partial_value, norm_part), "feat")
        squares = jnp.sum((margins - wanted) ** 2)
        dual_sum = jnp.sum(duals * wanted - 0.5 * duals * duals)
        local_stats = jnp.stack([squares, dual_sum, norm_feat / groups])
        collected.append(by_axis(local_stats, SAMP))
    totals = jnp.stack(collected)
    primal_value = totals[:, 0] / (2.0 * sample_total) + 0.5 * ridge * totals[:, 2]
    dual_value = totals[:, 1] / sample_total - 0.5 * ridge * totals[:, 2]
    objectives = jnp.stack([primal_value, dual_value], axis=1)
    restored = jnp.zeros_like(duals).at[block_order].set(duals)
    return (weights, restored, objectives)


def solution(mesh):
    torus = Mesh(mesh.devices.reshape(4, 8, mesh.shape["feat"]), ("samp_0", "samp_1", "feat"))
    in_specs = (P(SAMP, None), P(None, "feat"), P("feat"), P(SAMP), P(SAMP))
    out_specs = (P("feat"), P(SAMP), P())
    return jax.shard_map(
        on_device, mesh=torus, in_specs=in_specs, out_specs=out_specs, check_vma=False
    )
```

profile of v0, /device:TPU:8, one launch (start us, length us, event | category | flops | bytes accessed | tf_op | source)
XLA Modules:
  0.0 408.3 jit_solution(11873493601887005186)
XLA Ops:
  0.6 0.8 compare_select_fusion
  1.4 1.3 copy.46
  2.7 6.2 %gather_fusion = bf16[2048,96]{1,0:T(8,128)(2,1)S(1)} fusion(bf16[2048,96]{1,0:T(8,128)(2,1)S(1)} %copy.46, s32[2048]{0:T(1024)S(1)} %get-tuple-element.93), kind=kCustom, calls=%fused_computation | custom fusion | bytes 794624 | tf_op jit(solution)/shard_map/gather | solution.py:76
  8.9 60.9 %multiply_convert_fusion = bf16[2048,2048]{1,0:T(8,128)(2,1)} fusion(bf16[2048,96]{1,0:T(8,128)(2,1)S(1)} %gather_fusion, bf16[96,2048]{1,0:T(8,128)(2,1)S(1)} %copy-done, f32[2048]{0:T(1024)} %param.9), kind=kOutput, calls=%fused_computation.5 | convolution fusion | flops 817889280 | bytes 9183232 | tf_op jit(solution)/shard_map/dot_general | solution.py:78
  69.8 9.5 %convolution_bitcast_fusion = f32[8,1,256,256]{3,2,1,0:T(8,128)} fusion(bf16[8,256,2048]{2,1,0:T(8,128)(2,1)} %bitcast.363), kind=kOutput, calls=%fused_computation.7 | convolution fusion | flops 2147483648 | bytes 10485760 | tf_op jit(solution)/shard_map/bid,bjd->bij/dot_general | solution.py:81
  79.3 5.9 %all-to-all-start = ((f32[8,1,256,256]{3,2,1,0:T(8,128)}), f32[8,1,256,256]{3,2,1,0:T(8,128)S(1)}, u32[]{:S(2)}, u32[]{:S(2)}) async-start(f32[8,1,256,256]{3,2,1,0:T(8,128)} %convolution_bitcast_fusion), calls=%async_computation | async-start | bytes 4194304 | tf_op jit(solution)/shard_map/all_to_all | solution.py:23
  85.2 11.8 %gather_fusion.1 = f32[2048]{0:T(1024)S(1)} fusion(f32[2048]{0:T(1024)S(1)} %copy-done.1, s32[2048]{0:T(1024)S(1)} %get-tuple-element.93), kind=kCustom, calls=%fused_computation.1 | custom fusion | bytes 24576 | tf_op jit(solution)/shard_map/gather | solution.py:77
  97.0 13.8 %all-to-all-done = f32[8,1,256,256]{3,2,1,0:T(8,128)S(1)} async-done(((f32[8,1,256,256]{3,2,1,0:T(8,128)}), f32[8,1,256,256]{3,2,1,0:T(8,128)S(1)}, u32[]{:S(2)}, u32[]{:S(2)}) %all-to-all-start) | async-done | bytes 2097184 | tf_op jit(solution)/shard_map/all_to_all | solution.py:23
  111.4 11.7 %custom-call.18 = f32[1,128,128]{2,1,0:T(8,128)S(1)} custom-call(f32[1,128,128]{2,1,0:T(8,128)S(1)} %cholesky.117), custom_call_target="Cholesky" | custom-call | tf_op jit(solution)/shard_map/jit(cholesky)/cholesky | solution.py:83
  123.1 9.8 %custom-call.19 = f32[1,1,128,128]{2,3,1,0:T(8,128)S(1)} custom-call(f32[1,1,128,128]{3,2,1,0:T(8,128)S(1)} %get-tuple-element.91), custom_call_target="InvertDiagBlocksLowerTriangular" | custom-call | tf_op jit(solution)/shard_map/jit(cholesky)/cholesky | solution.py:83
  133.4 11.7 %custom-call.20 = f32[1,128,128]{2,1,0:T(8,128)S(1)} custom-call(f32[1,128,128]{2,1,0:T(8,128)S(1)} %fusion), custom_call_target="Cholesky" | custom-call | tf_op jit(solution)/shard_map/jit(cholesky)/cholesky | solution.py:83
  145.2 0.6 compare_reduce_fusion
  147.2 4.0 while.8
  147.8 1.4 bitcast_dynamic-update-slice_fusion.3
  149.8 1.4 bitcast_dynamic-update-slice_fusion.3
  151.2 19.9 %custom-call.24 = f32[1,2,128,128]{2,3,1,0:T(8,128)S(1)} custom-call(f32[1,2,128,128]{3,2,1,0:T(8,128)S(1)} %bitcast.391), custom_call_target="InvertDiagBlocksLowerTriangular" | custom-call | tf_op jit(solution)/shard_map/vmap(jit(_cho_solve))/triangular_solve | solution.py:64
  172.3 7.7 %all_to_all.73 = f32[8,1,256]{2,1,0:T(1,128)S(1)} all-to-all(f32[8,1,256]{2,1,0:T(1,128)S(1)} %broadcast_in_dim.54), channel_id=1, replica_groups=mesh['samp_0'=4,'samp_1'=8,'feat'=8] {'feat'}, dimensions={0} | all-to-all | bytes 16384 | tf_op jit(solution)/shard_map/all_to_all | solution.py:29
  180.0 4.6 %fusion.64 = f32[1,2048]{1,0:T(1,128)S(1)} fusion(bf16[2048,1]{0,1:T(2,128)(2,1)S(1)} %bitcast.364, bf16[2048,2048]{1,0:T(8,128)(2,1)} %multiply_convert_fusion), kind=kOutput, calls=%fused_computation.160 | convolution fusion | flops 8388608 | bytes 8400896 | tf_op jit(solution)/shard_map/dot_general | solution.py:96
  184.7 22.8 %all_to_all.74 = f32[32,1,2048]{2,1,0:T(1,128)S(1)} all-to-all(f32[32,1,2048]{2,1,0:T(1,128)S(1)} %broadcast_in_dim.55), channel_id=1, replica_groups=mesh['samp_0'=4,'samp_1'=8,'feat'=8] {'samp_0','samp_1'}, dimensions={0} | all-to-all | bytes 524288 | tf_op jit(solution)/shard_map/all_to_all | solution.py:29
  207.7 0.6 fusion.63
  208.3 5.6 %fusion.65 = f32[1,2048]{1,0:T(1,128)S(1)} fusion(bf16[2048,2048]{1,0:T(8,128)(2,1)} %multiply_convert_fusion, bf16[2048,1]{0,1:T(2,128)(2,1)S(1)} %reshape.387), kind=kOutput, calls=%fused_computation.161 | convolution fusion | flops 8388608 | bytes 8400896 | tf_op jit(solution)/shard_map/dot_general | solution.py:100
  213.9 0.7 pad_maximum_fusion
  214.6 0.7 broadcast_in_dim.56
  215.3 4.7 %all-to-all-start.3 = ((f32[8,1,2049]{2,1,0:T(1,128)}), f32[8,1,2049]{2,1,0:T(1,128)S(1)}, u32[]{:S(2)}, u32[]{:S(2)}) async-start(f32[8,1,2049]{2,1,0:T(1,128)} %broadcast_in_dim.56), calls=%async_computation.3 | async-start | bytes 139264 | tf_op jit(solution)/shard_map/all_to_all | solution.py:29
  220.0 4.2 %all-to-all-done.3 = f32[8,1,2049]{2,1,0:T(1,128)S(1)} async-done(((f32[8,1,2049]{2,1,0:T(1,128)}), f32[8,1,2049]{2,1,0:T(1,128)S(1)}, u32[]{:S(2)}, u32[]{:S(2)}) %all-to-all-start.3) | async-done | bytes 65600 | tf_op jit(solution)/shard_map/all_to_all | solution.py:29
  225.5 7.7 %all_to_all.75 = f32[8,1,256]{2,1,0:T(1,128)S(1)} all-to-all(f32[8,1,256]{2,1,0:T(1,128)S(1)} %broadcast_in_dim.57), channel_id=1, replica_groups=mesh['samp_0'=4,'samp_1'=8,'feat'=8] {'feat'}, dimensions={0} | all-to-all | bytes 16384 | tf_op jit(solution)/shard_map/all_to_all | solution.py:29
  233.2 4.6 %fusion.66 = f32[1,2048]{1,0:T(1,128)S(1)} fusion(bf16[2048,1]{0,1:T(2,128)(2,1)S(1)} %bitcast.365, bf16[2048,2048]{1,0:T(8,128)(2,1)} %multiply_convert_fusion), kind=kOutput, calls=%fused_computation.162 | convolution fusion | flops 8388608 | bytes 8400896 | tf_op jit(solution)/shard_map/dot_general | solution.py:96
  237.9 16.6 %all_to_all.76 = f32[32,1,2048]{2,1,0:T(1,128)S(1)} all-to-all(f32[32,1,2048]{2,1,0:T(1,128)S(1)} %broadcast_in_dim.58), channel_id=1, replica_groups=mesh['samp_0'=4,'samp_1'=8,'feat'=8] {'samp_0','samp_1'}, dimensions={0} | all-to-all | bytes 524288 | tf_op jit(solution)/shard_map/all_to_all | solution.py:29
  254.7 5.6 %fusion.67 = f32[1,2048]{1,0:T(1,128)S(1)} fusion(bf16[2048,2048]{1,0:T(8,128)(2,1)} %multiply_convert_fusion, bf16[2048,1]{0,1:T(2,128)(2,1)S(1)} %reshape.403), kind=kOutput, calls=%fused_computation.163 | convolution fusion | flops 8388608 | bytes 8400896 | tf_op jit(solution)/shard_map/dot_general | solution.py:100
  260.4 0.6 multiply_reduce_fusion.5
  261.0 0.6 pad_maximum_fusion.1
  261.6 0.7 broadcast_in_dim.59
  262.3 4.7 %all-to-all-start.6 = ((f32[8,1,2049]{2,1,0:T(1,128)}), f32[8,1,2049]{2,1,0:T(1,128)S(1)}, u32[]{:S(2)}, u32[]{:S(2)}) async-start(f32[8,1,2049]{2,1,0:T(1,128)} %broadcast_in_dim.59), calls=%async_computation.6 | async-start | bytes 139264 | tf_op jit(solution)/shard_map/all_to_all | solution.py:29
  267.0 4.2 %all-to-all-done.6 = f32[8,1,2049]{2,1,0:T(1,128)S(1)} async-done(((f32[8,1,2049]{2,1,0:T(1,128)}), f32[8,1,2049]{2,1,0:T(1,128)S(1)}, u32[]{:S(2)}, u32[]{:S(2)}) %all-to-all-start.6) | async-done | bytes 65600 | tf_op jit(solution)/shard_map/all_to_all | solution.py:29
  272.5 7.9 %all_to_all.77 = f32[8,1,256]{2,1,0:T(1,128)S(1)} all-to-all(f32[8,1,256]{2,1,0:T(1,128)S(1)} %broadcast_in_dim.60), channel_id=1, replica_groups=mesh['samp_0'=4,'samp_1'=8,'feat'=8] {'feat'}, dimensions={0} | all-to-all | bytes 16384 | tf_op jit(solution)/shard_map/all_to_all | solution.py:29
  280.5 4.6 %fusion.68 = f32[1,2048]{1,0:T(1,128)S(1)} fusion(bf16[2048,1]{0,1:T(2,128)(2,1)S(1)} %bitcast.366, bf16[2048,2048]{1,0:T(8,128)(2,1)} %multiply_convert_fusion), kind=kOutput, calls=%fused_computation.164 | convolution fusion | flops 8388608 | bytes 8400896 | tf_op jit(solution)/shard_map/dot_general | solution.py:96
  285.2 16.6 %all_to_all.78 = f32[32,1,2048]{2,1,0:T(1,128)S(1)} all-to-all(f32[32,1,2048]{2,1,0:T(1,128)S(1)} %broadcast_in_dim.61), channel_id=1, replica_groups=mesh['samp_0'=4,'samp_1'=8,'feat'=8] {'samp_0','samp_1'}, dimensions={0} | all-to-all | bytes 524288 | tf_op jit(solution)/shard_map/all_to_all | solution.py:29
  302.0 5.6 %fusion.69 = f32[1,2048]{1,0:T(1,128)S(1)} fusion(bf16[2048,2048]{1,0:T(8,128)(2,1)} %multiply_convert_fusion, bf16[2048,1]{0,1:T(2,128)(2,1)S(1)} %reshape.419), kind=kOutput, calls=%fused_computation.165 | convolution fusion | flops 8388608 | bytes 8400896 | tf_op jit(solution)/shard_map/dot_general | solution.py:100
  307.7 0.6 multiply_reduce_fusion.4
  308.3 0.6 pad_maximum_fusion.2
  308.9 0.7 broadcast_in_dim.62
  309.6 4.7 %all-to-all-start.9 = ((f32[8,1,2049]{2,1,0:T(1,128)}), f32[8,1,2049]{2,1,0:T(1,128)S(1)}, u32[]{:S(2)}, u32[]{:S(2)}) async-start(f32[8,1,2049]{2,1,0:T(1,128)} %broadcast_in_dim.62), calls=%async_computation.9 | async-start | bytes 139264 | tf_op jit(solution)/shard_map/all_to_all | solution.py:29
  314.3 4.2 %all-to-all-done.9 = f32[8,1,2049]{2,1,0:T(1,128)S(1)} async-done(((f32[8,1,2049]{2,1,0:T(1,128)}), f32[8,1,2049]{2,1,0:T(1,128)S(1)}, u32[]{:S(2)}, u32[]{:S(2)}) %all-to-all-start.9) | async-done | bytes 65600 | tf_op jit(solution)/shard_map/all_to_all | solution.py:29
  319.8 7.7 %all_to_all.79 = f32[8,1,256]{2,1,0:T(1,128)S(1)} all-to-all(f32[8,1,256]{2,1,0:T(1,128)S(1)} %broadcast_in_dim.63), channel_id=1, replica_groups=mesh['samp_0'=4,'samp_1'=8,'feat'=8] {'feat'}, dimensions={0} | all-to-all | bytes 16384 | tf_op jit(solution)/shard_map/all_to_all | solution.py:29
  327.5 4.6 %fusion.70 = f32[1,2048]{1,0:T(1,128)S(1)} fusion(bf16[2048,1]{0,1:T(2,128)(2,1)S(1)} %bitcast.367, bf16[2048,2048]{1,0:T(8,128)(2,1)} %multiply_convert_fusion), kind=kOutput, calls=%fused_computation.166 | convolution fusion | flops 8388608 | bytes 8400896 | tf_op jit(solution)/shard_map/dot_general | solution.py:96
  332.1 0.9 broadcast_in_dim.64
  332.9 4.4 %all-to-all-start.11 = ((f32[32,1,2048]{2,1,0:T(1,128)}), f32[32,1,2048]{2,1,0:T(1,128)S(1)}, u32[]{:S(2)}, u32[]{:S(2)}) async-start(f32[32,1,2048]{2,1,0:T(1,128)} %broadcast_in_dim.64), calls=%async_computation.11 | async-start | bytes 524288 | tf_op jit(solution)/shard_map/all_to_all | solution.py:29
  340.9 0.6 fusion.33
  341.5 8.3 %all-to-all-done.11 = f32[32,1,2048]{2,1,0:T(1,128)S(1)} async-done(((f32[32,1,2048]{2,1,0:T(1,128)}), f32[32,1,2048]{2,1,0:T(1,128)S(1)}, u32[]{:S(2)}, u32[]{:S(2)}) %all-to-all-start.11) | async-done | bytes 262176 | tf_op jit(solution)/shard_map/all_to_all | solution.py:29
  350.0 5.6 %fusion.71 = f32[1,2048]{1,0:T(1,128)S(1)} fusion(bf16[2048,2048]{1,0:T(8,128)(2,1)} %multiply_convert_fusion, bf16[2048,1]{0,1:T(2,128)(2,1)S(1)} %reshape.435), kind=kOutput, calls=%fused_computation.167 | convolution fusion | flops 8388608 | bytes 8400896 | tf_op jit(solution)/shard_map/dot_general | solution.py:100
  355.6 0.7 multiply_reduce_fusion
  356.3 0.7 pad_maximum_fusion.3
  357.0 0.7 broadcast_in_dim.66
  357.7 4.7 %all-to-all-start.12 = ((f32[8,1,2049]{2,1,0:T(1,128)}), f32[8,1,2049]{2,1,0:T(1,128)S(1)}, u32[]{:S(2)}, u32[]{:S(2)}) async-start(f32[8,1,2049]{2,1,0:T(1,128)} %broadcast_in_dim.66), calls=%async_computation.12 | async-start | bytes 139264 | tf_op jit(solution)/shard_map/all_to_all | solution.py:29
  362.4 4.2 %all-to-all-done.12 = f32[8,1,2049]{2,1,0:T(1,128)S(1)} async-done(((f32[8,1,2049]{2,1,0:T(1,128)}), f32[8,1,2049]{2,1,0:T(1,128)S(1)}, u32[]{:S(2)}, u32[]{:S(2)}) %all-to-all-start.12) | async-done | bytes 65600 | tf_op jit(solution)/shard_map/all_to_all | solution.py:29
  366.7 0.7 multiply_reduce_fusion.3
  368.5 1.3 pad_maximum_fusion.10
  369.8 1.3 pad_maximum_fusion.11
  371.0 1.4 pad_maximum_fusion.12
  372.4 1.4 pad_maximum_fusion.13
  373.8 8.6 %scatter_custom_fusion = f32[2048]{0:T(1024)} fusion(s32[2048]{0:T(1024)S(1)} %get-tuple-element.92, f32[2048]{0:T(1024)S(1)} %bitcast.378, f32[]{:T(128)} %constant.117.clone.1), kind=kCustom, calls=%fused_computation.102 | custom fusion | bytes 8196 | tf_op jit(solution)/shard_map/scatter | solution.py:110
  382.4 8.9 %all-reduce.2 = (f32[3]{0:T(128)S(1)}, f32[3]{0:T(128)S(1)}, f32[3]{0:T(128)S(1)}, f32[3]{0:T(128)S(1)}) all-reduce(f32[3]{0:T(128)S(1)} %pad_maximum_fusion.13, f32[3]{0:T(128)S(1)} %pad_maximum_fusion.12, f32[3]{0:T(128)S(1)} %pad_maximum_fusion.11, ...), channel_id=1, replica_groups=mesh['samp_0'=4,'samp_1'=8,'feat'=8] {'samp_0'}, use_global_device_ids=true, to_apply=%region_32.34 | all-reduce | flops 12 | bytes 96 | tf_op jit(solution)/shard_map/psum | solution.py:59
  391.3 15.8 %all-reduce.1 = (f32[1,3]{1,0:T(1,128)S(1)}, f32[1,3]{1,0:T(1,128)S(1)}, f32[1,3]{1,0:T(1,128)S(1)}, f32[1,3]{1,0:T(1,128)S(1)}) all-reduce(f32[1,3]{1,0:T(1,128)S(1)} %bitcast.387, f32[1,3]{1,0:T(1,128)S(1)} %bitcast.388, f32[1,3]{1,0:T(1,128)S(1)} %bitcast.389, ...), channel_id=1, replica_groups=mesh['samp_0'=4,'samp_1'=8,'feat'=8] {'samp_1'}, use_global_device_ids=true, to_apply=%region_33.35 | all-reduce | flops 12 | bytes 96 | tf_op jit(solution)/shard_map/psum | solution.py:59
  407.2 0.7 copy.66
  (107 shorter events, 10.9 us)
Async XLA Ops:
  0.6 8.2 %copy-start = (bf16[96,2048]{1,0:T(8,128)(2,1)S(1)}, bf16[96,2048]{1,0:T(8,128)(2,1)}, u32[]{:S(2)}) copy-start(bf16[96,2048]{1,0:T(8,128)(2,1)} %param.8) | copy-start | bytes 1179652
  69.8 15.4 %copy-start.1 = (f32[2048]{0:T(1024)S(1)}, f32[2048]{0:T(1024)}, u32[]{:S(2)}) copy-start(f32[2048]{0:T(1024)} %param.10) | copy-start | bytes 24580
  79.3 31.6 %all-to-all-start = ((f32[8,1,256,256]{3,2,1,0:T(8,128)}), f32[8,1,256,256]{3,2,1,0:T(8,128)S(1)}, u32[]{:S(2)}, u32[]{:S(2)}) async-start(f32[8,1,256,256]{3,2,1,0:T(8,128)} %convolution_bitcast_fusion), calls=%async_computation | async-start | bytes 4194304 | tf_op jit(solution)/shard_map/all_to_all | solution.py:23
  215.3 8.9 %all-to-all-start.3 = ((f32[8,1,2049]{2,1,0:T(1,128)}), f32[8,1,2049]{2,1,0:T(1,128)S(1)}, u32[]{:S(2)}, u32[]{:S(2)}) async-start(f32[8,1,2049]{2,1,0:T(1,128)} %broadcast_in_dim.56), calls=%async_computation.3 | async-start | bytes 139264 | tf_op jit(solution)/shard_map/all_to_all | solution.py:29
  262.3 8.9 %all-to-all-start.6 = ((f32[8,1,2049]{2,1,0:T(1,128)}), f32[8,1,2049]{2,1,0:T(1,128)S(1)}, u32[]{:S(2)}, u32[]{:S(2)}) async-start(f32[8,1,2049]{2,1,0:T(1,128)} %broadcast_in_dim.59), calls=%async_computation.6 | async-start | bytes 139264 | tf_op jit(solution)/shard_map/all_to_all | solution.py:29
  309.6 8.9 %all-to-all-start.9 = ((f32[8,1,2049]{2,1,0:T(1,128)}), f32[8,1,2049]{2,1,0:T(1,128)S(1)}, u32[]{:S(2)}, u32[]{:S(2)}) async-start(f32[8,1,2049]{2,1,0:T(1,128)} %broadcast_in_dim.62), calls=%async_computation.9 | async-start | bytes 139264 | tf_op jit(solution)/shard_map/all_to_all | solution.py:29
  332.9 16.8 %all-to-all-start.11 = ((f32[32,1,2048]{2,1,0:T(1,128)}), f32[32,1,2048]{2,1,0:T(1,128)S(1)}, u32[]{:S(2)}, u32[]{:S(2)}) async-start(f32[32,1,2048]{2,1,0:T(1,128)} %broadcast_in_dim.64), calls=%async_computation.11 | async-start | bytes 524288 | tf_op jit(solution)/shard_map/all_to_all | solution.py:29
  350.0 57.9 %copy-start.2 = (f32[2048]{0:T(1024)}, f32[2048]{0:T(1024)S(1)}, u32[]{:S(2)}) copy-start(f32[2048]{0:T(1024)S(1)} %get-tuple-element.81) | copy-start | bytes 24580
  357.7 8.9 %all-to-all-start.12 = ((f32[8,1,2049]{2,1,0:T(1,128)}), f32[8,1,2049]{2,1,0:T(1,128)S(1)}, u32[]{:S(2)}, u32[]{:S(2)}) async-start(f32[8,1,2049]{2,1,0:T(1,128)} %broadcast_in_dim.66), calls=%async_computation.12 | async-start | bytes 139264 | tf_op jit(solution)/shard_map/all_to_all | solution.py:29
where the time goes:
time: 414 us; the launch traced here: 408 us
  matrix products  116 us (28%)
  blocking collectives  112 us (27%)
  other arithmetic  67.8 us (16%)
  local copies, waits for them, and re-layouts  39.1 us (9%)
  waiting for transfers between devices  38.9 us (9%)
  starting transfers between devices  29.1 us (7%)
  between operations  5.41 us (1%)
    all_to_all x7, blocking collectives, from_everyone(): return lax.all_to_all(copies, axis, split_axis=0, concat_axis=0, tiled=True)  86.9 us
    dot_general x1, matrix products, on_device(): angles = jnp.dot(picked, frequencies, preferred_element_type=jnp.float32)  60.9 us
    another operation x6, other arithmetic, on_device(): factors = jnp.linalg.cholesky(gram_sums + jnp.eye(BLOCK, dtype=jnp.float32))  34 us
    all_to_all x5, waiting for transfers between devices, from_everyone(): return lax.all_to_all(copies, axis, split_axis=0, concat_axis=0, tiled=True)  25.1 us
    psum x2, blocking collectives, by_axis(): value = lax.psum(value, axis)  24.6 us
    all_to_all x5, starting transfers between devices, from_everyone(): return lax.all_to_all(copies, axis, split_axis=0, concat_axis=0, tiled=True)  23.3 us
    dot_general x4, matrix products, on_device(): jnp.dot(features, weight_bf, preferred_element_type=jnp.float32)  22.6 us
    another operation x8, other arithmetic, solve_block(): return jax.scipy.linalg.cho_solve((factor, True), vector)  20 us
  transfers between devices with their start and end apart: 6, of which 6 were waited for; matrix products, arithmetic and copies ran while one was open for 3% of the time, Pallas kernels for 0%

commit v1 on v0

v1 whole, which is shorter than its diff:
```python
import functools
import math

import jax
import jax.numpy as jnp
from jax import lax
from jax.experimental import pallas as pl
from jax.experimental.pallas import tpu as pltpu
from jax.sharding import Mesh
from jax.sharding import PartitionSpec as P

BLOCK = 256
ROUNDS = 4
PIECES = 4
MESH = pl.DeviceIdType.MESH
HIGHEST = lax.Precision.HIGHEST
F32 = jnp.float32
BF16 = jnp.bfloat16

SINE = (
    6.283185273782525,
    -41.341677476882325,
    81.60223116950678,
    -76.57499088229173,
    39.71091059155359,
)
TOP_EIGENVALUE = 519.0


def newton_schedule():
    rho = (TOP_EIGENVALUE - 1.0) / (TOP_EIGENVALUE + 1.0)
    scales = []
    while rho > 1e-4:
        scale = 2.0 / (2.0 - rho * rho)
        rho = rho * rho * scale / 2.0
        scales.append(scale)
    return scales


def dot(a, b, precision=None):
    return lax.dot_general(
        a, b, (((1,), (0,)), ((), ())), precision=precision, preferred_element_type=F32
    )


def dot_t(a, b):
    return lax.dot_general(a, b, (((1,), (1,)), ((), ())), preferred_element_type=F32)


def three_rows(value, rows):
    high = value.astype(BF16).astype(F32)
    middle = (value - high).astype(BF16).astype(F32)
    low = value - high - middle
    shape = (rows, value.shape[1])
    row = lax.broadcasted_iota(jnp.int32, shape, 0)
    tile = jnp.where(row == 0, high, jnp.where(row == 1, middle, jnp.where(row == 2, low, 0.0)))
    return tile.astype(BF16)


def kernel(
    sizes,
    order_s,
    inputs_ref,
    freq_ref,
    phase_ref,
    target_ref,
    order_ref,
    weights_out,
    duals_out,
    objectives_out,
    inputs_f,
    picked_f,
    picked_b,
    chosen,
    freq,
    phases,
    phi,
    gram,
    pair,
    inverse,
    rs_send,
    rs_recv,
    x_buf,
    z_buf,
    ag_buf,
    dual_buf,
    stat_f,
    stat_x,
    stat_z,
    sem_piece,
    sem_phase,
    sem_rs,
    sem_x,
    sem_z,
    sem_ag,
    sem_dual,
    sem_stat_f,
    sem_stat_x,
    sem_stat_z,
    out_right,
    out_left,
    out_relay,
    out_partner,
    out_phase,
    out_rs,
    out_x,
    out_z,
    out_ag,
    out_dual,
    out_stat_f,
    out_stat_x,
    out_stat_z,
):
    nx, nz, ny, nc = sizes
    nf = ny * nc
    rows = inputs_ref.shape[0]
    raw = inputs_ref.shape[1]
    width = freq_ref.shape[1]
    total_features = width * nf
    total_samples = rows * nx * nz
    piece = width // PIECES
    step_scale = BLOCK / total_samples
    ridge = 1.0 / BLOCK
    mx, mz = lax.axis_index("x"), lax.axis_index("z")
    my, mc = lax.axis_index("y"), lax.axis_index("core")
    me = my * nc + mc

    def feat_at(dy, dc):
        y = lax.rem(my + dy, ny)
        c = lax.rem(mc + dc, nc)
        return y, c, y * nc + c

    others = sorted(
        [(dy, dc) for dy in range(ny) for dc in range(nc) if (dy, dc) != (0, 0)],
        key=lambda o: (-min(o[0], ny - o[0]), o[1]),
    )

    barrier = pltpu.get_barrier_semaphore()
    for dy, dc in others:
        y, c, _ = feat_at(dy, dc)
        pl.semaphore_signal(barrier, inc=1, device_id={"y": y, "core": c}, device_id_type=MESH)
    for d in range(1, nx):
        pl.semaphore_signal(
            barrier, inc=1, device_id={"x": lax.rem(mx + d, nx)}, device_id_type=MESH
        )
    for d in range(1, nz):
        pl.semaphore_signal(
            barrier, inc=1, device_id={"z": lax.rem(mz + d, nz)}, device_id_type=MESH
        )

    lane = lax.broadcasted_iota(jnp.int32, (rows, 128), 1)
    inputs_f[...] = jnp.where((lane >= raw) & (lane < raw + 3), 1.0, 0.0)
    inputs_f[:, 0:raw] = inputs_ref[...].astype(F32)
    base = me * BLOCK

    def pick(i, _):
        picked_f[pl.ds(i, 1), :] = inputs_f[pl.ds(order_s[base + i], 1), :]
        return 0

    lax.fori_loop(0, BLOCK, pick, 0, unroll=8)
    picked_b[...] = picked_f[...].astype(BF16)

    pl.semaphore_wait(barrier, len(others) + nx - 1 + nz - 1)

    def send(src, dst, out_sem, in_sem, device):
        copy = pltpu.make_async_remote_copy(
            src_ref=src,
            dst_ref=dst,
            send_sem=out_sem,
            recv_sem=in_sem,
            device_id=device,
            device_id_type=MESH,
        )
        copy.start()
        return copy

    def cols(q):
        return pl.ds(pl.multiple_of(q * piece, piece), piece)

    def freq_piece(shard, q):
        return freq.at[shard, pl.ds(0, raw), cols(q)]

    y_right, _, from_right = feat_at(1, 0)
    y_left, _, from_left = feat_at(ny - 1, 0)
    partner = {"core": lax.rem(mc + 1, nc)}
    half = PIECES // 2
    started = []
    for i in range(PIECES):
        q, p = i, (i + half) % PIECES
        started.append(
            send(
                freq_ref.at[:, pl.ds(q * piece, piece)],
                freq_piece(me, q),
                out_right.at[q],
                sem_piece.at[me, q],
                {"y": y_right},
            )
        )
        started.append(
            send(
                freq_ref.at[:, pl.ds(p * piece, piece)],
                freq_piece(me, p),
                out_left.at[p],
                sem_piece.at[me, p],
                {"y": y_left},
            )
        )
        started.append(
            send(
                freq_ref.at[:, pl.ds(q * piece, piece)],
                freq_piece(me, q),
                out_partner.at[me, q],
                sem_piece.at[me, q],
                partner,
            )
        )
    for k, (dy, dc) in enumerate(reversed(others)):
        y, c, _ = feat_at(dy, dc)
        started.append(
            send(
                phase_ref,
                phases.at[me],
                out_phase.at[k],
                sem_phase.at[me],
                {"y": y, "core": c},
            )
        )
    freq[me, 0:raw, :] = freq_ref[...]
    phases[me] = phase_ref[...]

    own_order = order_ref[:, pl.ds(pl.multiple_of(base, BLOCK), BLOCK)]
    for part in range(rows // BLOCK):
        sample = lax.broadcasted_iota(jnp.int32, (BLOCK, BLOCK), 0) + part * BLOCK
        chosen[part * BLOCK : (part + 1) * BLOCK, :] = jnp.where(
            sample == own_order, 1.0, 0.0
        ).astype(BF16)
    wanted = jnp.sum(dot(three_rows(target_ref[...], 16), chosen[...]), axis=0, keepdims=True)

    def arrived(shard, q):
        pltpu.make_async_remote_copy(
            src_ref=freq_piece(shard, q),
            dst_ref=freq_piece(shard, q),
            send_sem=out_relay.at[0],
            recv_sem=sem_piece.at[shard, q],
            device_id=partner,
            device_id_type=MESH,
        ).wait_recv()

    amplitude = math.sqrt(2.0 / total_features)
    coefs = [-amplitude * v for v in SINE]
    gram[...] = jnp.zeros_like(gram)

    def make_piece(shard, q):
        freq[shard, raw:128, cols(q)] = three_rows(phases[shard, :, cols(q)], 128 - raw)
        angles = dot(picked_b[...], freq[shard, :, cols(q)])
        turns = angles * (0.5 / math.pi)
        wave = jnp.abs(turns - jnp.round(turns)) - 0.25
        square = wave * wave
        value = coefs[4]
        for c in (coefs[3], coefs[2], coefs[1], coefs[0]):
            value = value * square + c
        made = (value * wave).astype(BF16)
        phi[:, pl.ds(pl.multiple_of(shard * width + q * piece, piece), piece)] = made
        gram[...] += dot_t(made, made)

    def phases_in(dy, dc):
        _, _, shard = feat_at(dy, dc)
        pltpu.make_async_remote_copy(
            src_ref=phase_ref,
            dst_ref=phases.at[shard],
            send_sem=out_phase.at[0],
            recv_sem=sem_phase.at[shard],
            device_id=partner,
            device_id_type=MESH,
        ).wait_recv()
        return shard

    def own_step(q, _):
        make_piece(me, q)
        return 0

    lax.fori_loop(0, PIECES, own_step, 0)
    shard_p = phases_in(0, 1)

    def partner_step(q, _):
        arrived(shard_p, q)
        make_piece(shard_p, q)
        return 0

    lax.fori_loop(0, PIECES, partner_step, 0)

    def forward(shard, q):
        send(
            freq_piece(shard, q),
            freq_piece(shard, q),
            out_partner.at[shard, q],
            sem_piece.at[shard, q],
            partner,
        )

    left = phases_in(ny - 1, 0)
    left_p = phases_in(ny - 1, 1)
    right = phases_in(1, 0)
    right_p = phases_in(1, 1)
    for i in range(PIECES):
        q, p = i, (i + half) % PIECES
        arrived(left, q)
        if i < half:
            send(freq_piece(left, q), freq_piece(left, q), out_relay.at[q], sem_piece.at[left, q], {"y": y_right})
        forward(left, q)
        arrived(right, p)
        if i < half:
            send(freq_piece(right, p), freq_piece(right, p), out_relay.at[p], sem_piece.at[right, p], {"y": y_left})
        forward(right, p)
        make_piece(left, q)
        make_piece(right, p)
        arrived(left_p, q)
        make_piece(left_p, q)
        arrived(right_p, p)
        make_piece(right_p, p)
    far = phases_in(2, 0)
    far_p = phases_in(2, 1)
    for i in range(half):
        for q in (i, i + half):
            arrived(far, q)
            forward(far, q)
            make_piece(far, q)
            arrived(far_p, q)
            make_piece(far_p, q)

    row = lax.broadcasted_iota(jnp.int32, (BLOCK, BLOCK), 0)
    eye = jnp.where(row == lax.broadcasted_iota(jnp.int32, (BLOCK, BLOCK), 1), 1.0, 0.0)
    scales = newton_schedule()
    first = 2.0 / (1.0 + TOP_EIGENVALUE)
    gram[...] += eye
    error = eye - first * gram[...]
    pair[0:BLOCK, :] = (scales[0] * first) * (eye + error)
    pair[BLOCK:, :] = (1.0 - scales[0]) * eye + scales[0] * dot(error, error, HIGHEST)

    def newton(k, _):
        scale = jnp.float32(scales[1])
        for n in range(2, len(scales)):
            scale = jnp.where(k == n, jnp.float32(scales[n]), scale)
        product = dot(pair[...], pair[BLOCK:, :], HIGHEST)
        pair[0:BLOCK, :] = scale * (pair[0:BLOCK, :] + product[0:BLOCK, :])
        pair[BLOCK:, :] = (1.0 - scale) * eye + scale * product[BLOCK:, :]
        return 0

    lax.fori_loop(1, len(scales), newton, 0)
    guess = pair[0:BLOCK, :]
    residual = eye - dot(gram[...], guess, HIGHEST)
    inverse[...] = guess + dot(guess, residual, HIGHEST)

    lanes = lax.broadcasted_iota(jnp.int32, (1, 128), 1)

    def exchange(buf, sem_in, sem_out, at, mine, count, axis):
        copies = []
        for d in range(1, count):
            copies.append(
                send(
                    buf.at[at, mine],
                    buf.at[at, mine],
                    sem_out.at[d],
                    sem_in.at[at, mine],
                    {axis: lax.rem(mine + d, count)},
                )
            )
        for d in range(1, count):
            source = lax.rem(mine + d, count)
            pltpu.make_async_remote_copy(
                src_ref=buf.at[at, source],
                dst_ref=buf.at[at, source],
                send_sem=sem_out.at[d],
                recv_sem=sem_in.at[at, source],
                device_id={axis: source},
                device_id_type=MESH,
            ).wait_recv()
        return copies

    def feat_wait(buf, sem_in, sem_out, at, dy, dc):
        y, c, source = feat_at(dy, dc)
        pltpu.make_async_remote_copy(
            src_ref=buf.at[at, source],
            dst_ref=buf.at[at, source],
            send_sem=sem_out.at[0],
            recv_sem=sem_in.at[at, source],
            device_id={"y": y, "core": c},
            device_id_type=MESH,
        ).wait_recv()
        return source

    def added(buf, at, count):
        value = buf[at, 0]
        for k in range(1, count):
            value = value + buf[at, k]
        return value

    def features_of(shard):
        return phi[:, pl.ds(pl.multiple_of(shard * width, width), width)]

    def spread(value, count):
        return jnp.broadcast_to(value, (count, value.shape[1]))

    def one_round(r, carry):
        alpha, margins, weights, stats = carry
        rest = spread(wanted - alpha - margins, 8)
        delta = dot(rest, inverse[...], HIGHEST)[0:1, :]
        alpha = alpha + delta
        delta_b = spread(delta, 16).astype(BF16)
        copies = []
        for k, (dy, dc) in enumerate(others):
            y, c, target = feat_at(dy, dc)
            rs_send[r, k] = dot(delta_b, features_of(target))[0:1, :] * step_scale
            copies.append(
                send(
                    rs_send.at[r, k],
                    rs_recv.at[r, me],
                    out_rs.at[k],
                    sem_rs.at[r, me],
                    {"y": y, "core": c},
                )
            )
        rs_recv[r, me] = dot(delta_b, features_of(me))[0:1, :] * step_scale
        for dy, dc in reversed(others):
            feat_wait(rs_recv, sem_rs, out_rs, r, dy, dc)
        part = added(rs_recv, r, nf)
        if nx > 1:
            x_buf[r, mx] = part
            copies += exchange(x_buf, sem_x, out_x, r, mx, nx, "x")
            part = added(x_buf, r, nx)
        if nz > 1:
            z_buf[r, mz] = part
            copies += exchange(z_buf, sem_z, out_z, r, mz, nz, "z")
            part = added(z_buf, r, nz)
        weights = weights + part
        ag_buf[r, me] = weights.astype(BF16).astype(F32)
        for k, (dy, dc) in enumerate(others):
            y, c, _ = feat_at(dy, dc)
            copies.append(
                send(
                    ag_buf.at[r, me],
                    ag_buf.at[r, me],
                    out_ag.at[k],
                    sem_ag.at[r, me],
                    {"y": y, "core": c},
                )
            )

        def margin_of(source):
            return dot_t(spread(ag_buf[r, source], 16).astype(BF16), features_of(source))

        total = margin_of(me)
        for dy, dc in reversed(others):
            total = total + margin_of(feat_wait(ag_buf, sem_ag, out_ag, r, dy, dc))
        margins = total[0:1, :]
        off = margins - wanted
        squares = jnp.sum(off * off, axis=1, keepdims=True)
        dual = jnp.sum(alpha * wanted - 0.5 * alpha * alpha, axis=1, keepdims=True)
        norm = jnp.sum(weights * weights, axis=1, keepdims=True) * (1.0 / (nx * nz))
        stats = jnp.where(lanes == r, squares, stats)
        stats = jnp.where(lanes == r + 8, dual, stats)
        stats = jnp.where(lanes == r + 16, norm, stats)
        for copy in copies:
            copy.wait_send()
        return alpha, margins, weights, stats

    zero = jnp.zeros((1, BLOCK), F32)
    alpha, _, weights, stats = lax.fori_loop(
        0,
        ROUNDS,
        one_round,
        (zero, zero, jnp.zeros((1, width), F32), jnp.zeros((1, 128), F32)),
    )

    copies = []
    stat_f[0, me] = stats
    for k, (dy, dc) in enumerate(others):
        y, c, _ = feat_at(dy, dc)
        copies.append(
            send(
                stat_f.at[0, me],
                stat_f.at[0, me],
                out_stat_f.at[k],
                sem_stat_f.at[0, me],
                {"y": y, "core": c},
            )
        )
    dual_buf[0, me] = jnp.sum(dot_t(three_rows(alpha, 16), chosen[...]), axis=0, keepdims=True)
    for k, (dy, dc) in enumerate(others):
        y, c, _ = feat_at(dy, dc)
        copies.append(
            send(
                dual_buf.at[0, me],
                dual_buf.at[0, me],
                out_dual.at[k],
                sem_dual.at[0, me],
                {"y": y, "core": c},
            )
        )
    weights_out[...] = weights
    for dy, dc in reversed(others):
        feat_wait(stat_f, sem_stat_f, out_stat_f, 0, dy, dc)
    stats = added(stat_f, 0, nf)
    if nx > 1:
        stat_x[0, mx] = stats
        copies += exchange(stat_x, sem_stat_x, out_stat_x, 0, mx, nx, "x")
        stats = added(stat_x, 0, nx)
    for dy, dc in reversed(others):
        feat_wait(dual_buf, sem_dual, out_dual, 0, dy, dc)
    duals_out[...] = added(dual_buf, 0, nf)
    if nz > 1:
        stat_z[0, mz] = stats
        copies += exchange(stat_z, sem_stat_z, out_stat_z, 0, mz, nz, "z")
        stats = added(stat_z, 0, nz)

    wide = jnp.broadcast_to(stats, (ROUNDS, 128))
    lane = lax.broadcasted_iota(jnp.int32, (ROUNDS, 128), 1)
    line = lax.broadcasted_iota(jnp.int32, (ROUNDS, 128), 0)

    def column(first):
        return jnp.sum(jnp.where(lane == line + first, wide, 0.0), axis=1, keepdims=True)

    squares, dual, norm = column(0), column(8), column(16)
    primal = squares / (2.0 * total_samples) + 0.5 * ridge * norm
    dual = dual / total_samples - 0.5 * ridge * norm
    side = lax.broadcasted_iota(jnp.int32, (ROUNDS, 2), 1)
    objectives_out[...] = jnp.where(side == 0, primal, dual)

    for copy in started + copies:
        copy.wait_send()
    for q in range(PIECES):
        for shard in (left, right, far):
            pltpu.make_async_remote_copy(
                src_ref=freq_piece(shard, q),
                dst_ref=freq_piece(shard, q),
                send_sem=out_partner.at[shard, q],
                recv_sem=sem_piece.at[shard, q],
                device_id=partner,
                device_id_type=MESH,
            ).wait_send()
        pltpu.make_async_remote_copy(
            src_ref=freq_piece(me, q),
            dst_ref=freq_piece(me, q),
            send_sem=out_relay.at[q],
            recv_sem=sem_piece.at[me, q],
            device_id=partner,
            device_id_type=MESH,
        ).wait_send()


def on_device(sizes, inputs, frequencies, phases, targets, block_order):
    nx, nz, ny, nc = sizes
    nf = ny * nc
    rows = inputs.shape[0]
    width = frequencies.shape[1]
    vmem = pl.BlockSpec(memory_space=pltpu.VMEM)
    dma = pltpu.SemaphoreType.DMA
    scratch = [
        pltpu.VMEM((rows, 128), F32),
        pltpu.VMEM((BLOCK, 128), F32),
        pltpu.VMEM((BLOCK, 128), BF16),
        pltpu.VMEM((rows, BLOCK), BF16),
        pltpu.VMEM((nf, 128, width), BF16),
        pltpu.VMEM((nf, 1, width), F32),
        pltpu.VMEM((BLOCK, nf * width), BF16),
        pltpu.VMEM((BLOCK, BLOCK), F32),
        pltpu.VMEM((2 * BLOCK, BLOCK), F32),
        pltpu.VMEM((BLOCK, BLOCK), F32),
        pltpu.VMEM((ROUNDS, nf, 1, width), F32),
        pltpu.VMEM((ROUNDS, nf, 1, width), F32),
        pltpu.VMEM((ROUNDS, nx, 1, width), F32),
        pltpu.VMEM((ROUNDS, nz, 1, width), F32),
        pltpu.VMEM((ROUNDS, nf, 1, width), F32),
        pltpu.VMEM((1, nf, 1, rows), F32),
        pltpu.VMEM((1, nf, 1, 128), F32),
        pltpu.VMEM((1, nx, 1, 128), F32),
        pltpu.VMEM((1, nz, 1, 128), F32),
        dma((nf, PIECES)),
        dma((nf,)),
        dma((ROUNDS, nf)),
        dma((ROUNDS, nx)),
        dma((ROUNDS, nz)),
        dma((ROUNDS, nf)),
        dma((1, nf)),
        dma((1, nf)),
        dma((1, nx)),
        dma((1, nz)),
        dma((PIECES,)),
        dma((PIECES,)),
        dma((PIECES,)),
        dma((nf, PIECES)),
        dma((nf,)),
        dma((nf,)),
        dma((nx,)),
        dma((nz,)),
        dma((nf,)),
        dma((nf,)),
        dma((nf,)),
        dma((nx,)),
        dma((nz,)),
    ]
    weights, duals, objectives = pl.pallas_call(
        functools.partial(kernel, sizes),
        out_shape=(
            jax.ShapeDtypeStruct((1, width), F32),
            jax.ShapeDtypeStruct((1, rows), F32),
            jax.ShapeDtypeStruct((ROUNDS, 2), F32),
        ),
        in_specs=[pl.BlockSpec(memory_space=pltpu.SMEM)] + [vmem] * 5,
        out_specs=(vmem, vmem, vmem),
        scratch_shapes=scratch,
        compiler_params=pltpu.CompilerParams(
            collective_id=0, has_side_effects=True, vmem_limit_bytes=60 * 1024 * 1024
        ),
        name="cocoa",
    )(
        block_order,
        inputs,
        frequencies,
        phases.reshape(1, width),
        targets.reshape(1, rows),
        block_order.reshape(1, rows),
    )
    return weights.reshape(width), duals.reshape(rows), objectives


def solution(mesh):
    devices = mesh.devices
    samp, feat = mesh.shape["samp"], mesh.shape["feat"]
    nc = 2
    ny = feat // nc
    nx = 4 if samp == 32 else 1
    nz = samp // nx
    torus = Mesh(devices.reshape(nx, nz, ny, nc), ("x", "z", "y", "core"))
    samp_axes, feat_axes = ("x", "z"), ("y", "core")
    in_specs = (
        P(samp_axes, None),
        P(None, feat_axes),
        P(feat_axes),
        P(samp_axes),
        P(samp_axes),
    )
    out_specs = (P(feat_axes), P(samp_axes), P())
    return jax.shard_map(
        functools.partial(on_device, (nx, nz, ny, nc)),
        mesh=torus,
        in_specs=in_specs,
        out_specs=out_specs,
        check_vma=False,
    )
```

time: 414 us -> 139 us (0.34); the launches traced: 408 us -> 139 us
  Pallas kernels: 0 us -> 134 us
  matrix products: 116 us -> 0 us
  blocking collectives: 112 us -> 0 us
  other arithmetic: 67.8 us -> 0 us
  waiting for transfers between devices: 38.9 us -> 0 us
  local copies, waits for them, and re-layouts: 39.1 us -> 4.62 us
  starting transfers between devices: 29.1 us -> 0 us
  between operations: 5.41 us -> 0.65 us
    pallas_call x0 -> x1, Pallas kernels: none -> 134 us  [on_device(): pl.pallas_call(functools.partial(kernel, sizes), out_shape=(jax.ShapeDtyp...]
    dot_general x10 -> x0, matrix products: 111 us -> none  [the longest x1 60.9 us: on_device(): angles = jnp.dot(picked, frequencies, preferred_element_type=jnp.float32)]
    all_to_all x7 -> x0, blocking collectives: 86.9 us -> none  [from_everyone(): return lax.all_to_all(copies, axis, split_axis=0, concat_axis=0, tiled=True)]
    another operation x20 -> x0, other arithmetic: 59.3 us -> none  [the longest x6 34 us: on_device(): factors = jnp.linalg.cholesky(gram_sums + jnp.eye(BLOCK, dtype=jnp.float32))]
    all_to_all x6 -> x0, waiting for transfers between devices: 38.9 us -> none  [the longest x5 25.1 us: from_everyone(): return lax.all_to_all(copies, axis, split_axis=0, concat_axis=0, tiled=True)]
    all_to_all x6 -> x0, starting transfers between devices: 29.1 us -> none  [the longest x5 23.3 us: from_everyone(): return lax.all_to_all(copies, axis, split_axis=0, concat_axis=0, tiled=True)]
    psum x2 -> x0, blocking collectives: 24.6 us -> none  [by_axis(): value = lax.psum(value, axis)]
    gather x3 -> x0, local copies, waits for them, and re-layouts: 18 us -> none  [the longest x2 11.8 us: on_device(): wanted = targets[block_order]]
  transfers between devices with their start and end apart: 6 -> 0, of which waited for: 6 -> 0; matrix products, arithmetic and copies ran while one was open for 3% -> 0% of each run, Pallas kernels for 0% -> 0%
where the time goes in v1:
time: 139 us
  Pallas kernels  134 us (96%)
  local copies, waits for them, and re-layouts  4.62 us (3%)
    pallas_call x1, Pallas kernels, on_device(): pl.pallas_call(functools.partial(kernel, sizes), out_shape=(jax.ShapeDtyp...  134 us
    unnamed x8, local copies, waits for them, and re-layouts  4.62 us

profile of v1, /device:TPU:8, one launch (start us, length us, event | category | flops | bytes accessed | tf_op | source)
XLA Modules:
  0.0 138.8 jit_solution(9001964599886854974)
XLA Ops:
  0.6 2.0 %copy.8.inputs_ref = bf16[2048,96]{1,0:T(8,128)(2,1)} copy(bf16[2048,96]{0,1:T(8,128)(2,1)} %param.5) | data formatting | bytes 786432 | tf_op args[0]
  2.6 133.6 %cocoa.1 = (f32[1,2048]{1,0:T(1,128)}, f32[1,2048]{1,0:T(1,128)}, f32[4,2]{1,0:T(4,128)}) custom-call(s32[2048]{0:T(1024)} %order_s.1, bf16[2048,96]{1,0:T(8,128)(2,1)} %copy.8.inputs_ref, bf16[96,2048]{1,0:T(8,128)(2,1)} %freq_ref.1, f32[1,2048]{1,0:T(1,128)} %bitcast.8, f32[1,2048]{1,0:T(1,128)} %bitcast.9, s32[1,2048]{1,0:T(1,128)} %bitcast.5), custom_call_target="tpu_custom_call" | custom-call | tf_op jit(solution)/shard_map/cocoa/pallas_call | solution.py:602
  136.2 0.0 copy-start.1
  136.2 1.3 copy.9
  137.5 0.0 copy-done.1
  137.5 0.0 copy-start
  137.5 0.6 copy.12
  138.1 0.1 copy-done
  138.2 0.6 copy.13
Async XLA Ops:
  136.2 1.3 copy-start.1
  137.5 0.7 copy-start

commit v2 on v1

v2 whole, which is shorter than its diff:
```python
import functools
import math

import jax
import jax.numpy as jnp
from jax import lax
from jax.experimental import pallas as pl
from jax.experimental.pallas import tpu as pltpu
from jax.sharding import Mesh
from jax.sharding import PartitionSpec as P

BLOCK = 256
ROUNDS = 4
PIECES = 4
MESH = pl.DeviceIdType.MESH
HIGHEST = lax.Precision.HIGHEST
F32 = jnp.float32
BF16 = jnp.bfloat16

SINE = (
    6.283185273782525,
    -41.341677476882325,
    81.60223116950678,
    -76.57499088229173,
    39.71091059155359,
)
TOP_EIGENVALUE = 519.0


def newton_schedule():
    rho = (TOP_EIGENVALUE - 1.0) / (TOP_EIGENVALUE + 1.0)
    scales = []
    while rho > 1e-4:
        scale = 2.0 / (2.0 - rho * rho)
        rho = rho * rho * scale / 2.0
        scales.append(scale)
    return scales


def dot(a, b, precision=None):
    return lax.dot_general(
        a, b, (((1,), (0,)), ((), ())), precision=precision, preferred_element_type=F32
    )


def dot_t(a, b):
    return lax.dot_general(a, b, (((1,), (1,)), ((), ())), preferred_element_type=F32)


def three_rows(value, rows):
    high = value.astype(BF16).astype(F32)
    middle = (value - high).astype(BF16).astype(F32)
    low = value - high - middle
    shape = (rows, value.shape[1])
    row = lax.broadcasted_iota(jnp.int32, shape, 0)
    tile = jnp.where(row == 0, high, jnp.where(row == 1, middle, jnp.where(row == 2, low, 0.0)))
    return tile.astype(BF16)


def kernel(
    sizes,
    inputs_ref,
    freq_ref,
    phase_ref,
    target_ref,
    order_ref,
    weights_out,
    duals_out,
    objectives_out,
    picked_b,
    chosen,
    freq,
    phases,
    phi,
    gram,
    gram_in,
    pair,
    inverse,
    delta_c,
    margin_c,
    rs_send,
    rs_recv,
    x_buf,
    z_buf,
    ag_buf,
    margin_buf,
    dual_buf,
    stat_y,
    stat_x,
    stat_z,
    sem_piece,
    sem_phase,
    sem_gram,
    sem_inverse,
    sem_rs,
    sem_x,
    sem_z,
    sem_ag,
    sem_margin,
    sem_dual,
    sem_stat_y,
    sem_stat_x,
    sem_stat_z,
    out_right,
    out_left,
    out_relay,
    out_phase,
    out_swap,
    out_rs,
    out_x,
    out_z,
    out_ag,
    out_margin,
    out_dual,
    out_stat_y,
    out_stat_x,
    out_stat_z,
):
    nx, nz, ny, nc = sizes
    raw, rows = inputs_ref.shape
    width = freq_ref.shape[1]
    total_features = width * ny * nc
    total_samples = rows * nx * nz
    held = nc * BLOCK
    piece = width // PIECES
    half = PIECES // 2
    step_scale = BLOCK / total_samples
    ridge = 1.0 / BLOCK
    mx, mz = lax.axis_index("x"), lax.axis_index("z")
    my, mc = lax.axis_index("y"), lax.axis_index("core")
    other = lax.rem(mc + 1, nc)
    partner = {"core": other}

    def y_at(d):
        return lax.rem(my + d, ny)

    y_far_first = sorted(range(1, ny), key=lambda d: (-min(d, ny - d), d))

    barrier = pltpu.get_barrier_semaphore()
    peers = [partner] + [{"y": y_at(d)} for d in y_far_first]
    peers += [{"x": lax.rem(mx + d, nx)} for d in range(1, nx)]
    peers += [{"z": lax.rem(mz + d, nz)} for d in range(1, nz)]
    for peer in peers:
        pl.semaphore_signal(barrier, inc=1, device_id=peer, device_id_type=MESH)

    own_order = order_ref[:, pl.ds(pl.multiple_of(my * held, held), held)]
    for part in range(rows // BLOCK):
        sample = lax.broadcasted_iota(jnp.int32, (BLOCK, held), 0) + part * BLOCK
        chosen[part * BLOCK : (part + 1) * BLOCK, :] = jnp.where(
            sample == own_order, 1.0, 0.0
        ).astype(BF16)
    line = lax.broadcasted_iota(jnp.int32, (128 - raw, held), 0)
    ones = jnp.where(line < 3, 1.0, 0.0)
    picked = jnp.concatenate([dot(inputs_ref[...], chosen[...]), ones], axis=0)
    picked_b[...] = jnp.transpose(picked).astype(BF16)

    pl.semaphore_wait(barrier, len(peers))

    def remote(src, dst, out_sem, in_sem, device):
        return pltpu.make_async_remote_copy(
            src_ref=src,
            dst_ref=dst,
            send_sem=out_sem,
            recv_sem=in_sem,
            device_id=device,
            device_id_type=MESH,
        )

    def send(*args):
        copy = remote(*args)
        copy.start()
        return copy

    def cols(q):
        return pl.ds(pl.multiple_of(q * piece, piece), piece)

    def freq_piece(shard, q):
        return freq.at[shard, pl.ds(0, raw), cols(q)]

    y_right, y_left, y_far = y_at(1), y_at(ny - 1), y_at(2)
    started = []
    for d in y_far_first:
        started.append(
            send(phase_ref, phases.at[my], out_phase.at[d], sem_phase.at[my], {"y": y_at(d)})
        )
    for i in range(PIECES):
        for q, out, y in ((i, out_right, y_right), ((i + half) % PIECES, out_left, y_left)):
            started.append(
                send(
                    freq_ref.at[:, pl.ds(q * piece, piece)],
                    freq_piece(my, q),
                    out.at[q],
                    sem_piece.at[my, q],
                    {"y": y},
                )
            )
    freq[my, 0:raw, :] = freq_ref[...]
    phases[my] = phase_ref[...]
    wanted = jnp.sum(dot(three_rows(target_ref[...], 16), chosen[...]), axis=0, keepdims=True)

    amplitude = math.sqrt(2.0 / total_features)
    coefs = [-amplitude * v for v in SINE]
    gram[...] = jnp.zeros_like(gram)

    def make_piece(shard, q):
        freq[shard, raw:128, cols(q)] = three_rows(phases[shard, :, cols(q)], 128 - raw)
        for b in range(nc):
            block = slice(b * BLOCK, (b + 1) * BLOCK)
            angles = dot(picked_b[block, :], freq[shard, :, cols(q)])
            turns = angles * (0.5 / math.pi)
            wave = jnp.abs(turns - jnp.round(turns)) - 0.25
            square = wave * wave
            value = coefs[4]
            for c in (coefs[3], coefs[2], coefs[1], coefs[0]):
                value = value * square + c
            made = (value * wave).astype(BF16)
            phi[block, pl.ds(pl.multiple_of(shard * width + q * piece, piece), piece)] = made
            gram[b] += dot_t(made, made)

    def own_step(q, _):
        make_piece(my, q)
        return 0

    lax.fori_loop(0, PIECES, own_step, 0)

    def arrived(shard, q):
        remote(
            freq_piece(shard, q),
            freq_piece(shard, q),
            out_relay.at[0],
            sem_piece.at[shard, q],
            {"y": y_left},
        ).wait_recv()

    def phases_in(shard):
        remote(
            phase_ref, phases.at[shard], out_phase.at[0], sem_phase.at[shard], {"y": y_left}
        ).wait_recv()

    def relay(shard, q, y):
        started.append(
            send(
                freq_piece(shard, q),
                freq_piece(shard, q),
                out_relay.at[q],
                sem_piece.at[shard, q],
                {"y": y},
            )
        )

    for shard in (y_left, y_right, y_far):
        phases_in(shard)
    for i in range(PIECES):
        q, p = i, (i + half) % PIECES
        arrived(y_left, q)
        if i < half:
            relay(y_left, q, y_right)
        arrived(y_right, p)
        if i < half:
            relay(y_right, p, y_left)
        make_piece(y_left, q)
        make_piece(y_right, p)
    for i in range(half):
        for q in (i, i + half):
            arrived(y_far, q)
            make_piece(y_far, q)

    swap = send(gram.at[other], gram_in, out_swap.at[0], sem_gram.at[0], partner)
    row = lax.broadcasted_iota(jnp.int32, (BLOCK, BLOCK), 0)
    eye = jnp.where(row == lax.broadcasted_iota(jnp.int32, (BLOCK, BLOCK), 1), 1.0, 0.0)
    swap.wait()
    gram_in[...] = gram[mc] + gram_in[...] + eye

    scales = newton_schedule()
    first = 2.0 / (1.0 + TOP_EIGENVALUE)
    error = eye - first * gram_in[...]
    pair[0:BLOCK, :] = (scales[0] * first) * (eye + error)
    pair[BLOCK:, :] = (1.0 - scales[0]) * eye + scales[0] * dot(error, error, HIGHEST)

    def newton(k, _):
        scale = jnp.float32(scales[1])
        for n in range(2, len(scales)):
            scale = jnp.where(k == n, jnp.float32(scales[n]), scale)
        product = dot(pair[...], pair[BLOCK:, :], HIGHEST)
        pair[0:BLOCK, :] = scale * (pair[0:BLOCK, :] + product[0:BLOCK, :])
        pair[BLOCK:, :] = (1.0 - scale) * eye + scale * product[BLOCK:, :]
        return 0

    lax.fori_loop(1, len(scales), newton, 0)
    guess = pair[0:BLOCK, :]
    residual = eye - dot(gram_in[...], guess, HIGHEST)
    inverse[mc] = guess + dot(guess, residual, HIGHEST)
    started.append(
        send(inverse.at[mc], inverse.at[mc], out_swap.at[1], sem_inverse.at[mc], partner)
    )
    remote(
        inverse.at[other], inverse.at[other], out_swap.at[1], sem_inverse.at[other], partner
    ).wait_recv()

    lanes = lax.broadcasted_iota(jnp.int32, (1, 128), 1)

    def exchange(buf, sem_in, sem_out, at, mine, count, axis):
        copies = []
        for d in range(1, count):
            copies.append(
                send(
                    buf.at[at, mine],
                    buf.at[at, mine],
                    sem_out.at[d],
                    sem_in.at[at, mine],
                    {axis: lax.rem(mine + d, count)},
                )
            )
        for d in range(1, count):
            source = lax.rem(mine + d, count)
            received(buf, sem_in, sem_out, at, source, {axis: source})
        return copies

    def received(buf, sem_in, sem_out, at, source, device):
        remote(
            buf.at[at, source],
            buf.at[at, source],
            sem_out.at[0],
            sem_in.at[at, source],
            device,
        ).wait_recv()

    def added(buf, at, count):
        value = buf[at, 0]
        for k in range(1, count):
            value = value + buf[at, k]
        return value

    group = min(512, width)

    def weigh(shard):
        done = []
        for g in range(width // group):
            at = pl.ds(pl.multiple_of(shard * width + g * group, group), group)
            total = jnp.zeros((16, group), F32)
            for t in range(held // 16):
                by = delta_c[t * 16 : (t + 1) * 16, :]
                by = jnp.concatenate([by] * (group // 128), axis=1)
                total = total + phi[t * 16 : (t + 1) * 16, at].astype(F32) * by
            done.append(jnp.sum(total, axis=0, keepdims=True))
        return jnp.concatenate(done, axis=1) * step_scale

    def add_margins(shard, weight):
        used = weight.astype(BF16).astype(F32)
        tall = 64

        def some_rows(t, _):
            at = pl.ds(pl.multiple_of(t * tall, tall), tall)
            total = margin_c[at, :]
            for g in range(width // 128):
                columns = pl.ds(pl.multiple_of(shard * width + g * 128, 128), 128)
                total = total + phi[at, columns].astype(F32) * used[:, g * 128 : (g + 1) * 128]
            margin_c[at, :] = total
            return 0

        lax.fori_loop(0, held // tall, some_rows, 0)

    def one_round(r, carry):
        alpha, margins, weights, squares_row, duals_row, norms = carry
        rest = wanted - alpha - margins
        parts = []
        for b in range(nc):
            block = inverse[b] * rest[:, b * BLOCK : (b + 1) * BLOCK]
            parts.append(jnp.sum(block, axis=1, keepdims=True))
        column = jnp.broadcast_to(jnp.concatenate(parts, axis=0), (held, 128))
        delta_c[...] = column.astype(BF16).astype(F32)
        copies = []
        for d in y_far_first:
            rs_send[r, d] = weigh(y_at(d))
            copies.append(
                send(
                    rs_send.at[r, d],
                    rs_recv.at[r, my],
                    out_rs.at[d],
                    sem_rs.at[r, my],
                    {"y": y_at(d)},
                )
            )
        rs_recv[r, my] = weigh(my)
        turned = jnp.concatenate(
            [
                jnp.transpose(column[t * 128 : (t + 1) * 128, :])[0:1, :]
                for t in range(held // 128)
            ],
            axis=1,
        )
        alpha = alpha + turned
        for d in range(1, ny):
            received(rs_recv, sem_rs, out_rs, r, y_at(d), {"y": y_at(d)})
        part = added(rs_recv, r, ny)
        if nx > 1:
            x_buf[r, mx] = part
            copies += exchange(x_buf, sem_x, out_x, r, mx, nx, "x")
            part = added(x_buf, r, nx)
        if nz > 1:
            z_buf[r, mz] = part
            copies += exchange(z_buf, sem_z, out_z, r, mz, nz, "z")
            part = added(z_buf, r, nz)
        weights = weights + part
        ag_buf[r, my] = weights
        for d in y_far_first:
            copies.append(
                send(
                    ag_buf.at[r, my],
                    ag_buf.at[r, my],
                    out_ag.at[d],
                    sem_ag.at[r, my],
                    {"y": y_at(d)},
                )
            )
        margin_c[...] = jnp.zeros_like(margin_c)
        add_margins(my, weights)
        for d in reversed(y_far_first):
            received(ag_buf, sem_ag, out_ag, r, y_at(d), {"y": y_at(d)})
            add_margins(y_at(d), ag_buf[r, y_at(d)])
        row = jnp.concatenate(
            [
                jnp.sum(
                    jnp.transpose(margin_c[t * 128 : (t + 1) * 128, :]), axis=0, keepdims=True
                )
                for t in range(held // 128)
            ],
            axis=1,
        )
        whole = ag_buf[r, 0] * ag_buf[r, 0]
        for k in range(1, ny):
            whole = whole + ag_buf[r, k] * ag_buf[r, k]
        norm = jnp.sum(whole, axis=1, keepdims=True)
        margin_buf[r, mc, :, 0:held] = row
        margin_buf[r, mc, :, held:] = jnp.broadcast_to(norm, (1, 128))
        copies.append(
            send(
                margin_buf.at[r, mc],
                margin_buf.at[r, mc],
                out_margin.at[0],
                sem_margin.at[r, mc],
                partner,
            )
        )
        received(margin_buf, sem_margin, out_margin, r, other, partner)
        both = added(margin_buf, r, nc)
        margins = both[:, 0:held]
        norms = jnp.where(lanes == r, both[:, held:], norms)
        off = margins - wanted
        squares = jnp.sum(off * off, axis=1, keepdims=True)
        dual = jnp.sum(alpha * wanted - 0.5 * alpha * alpha, axis=1, keepdims=True)
        squares_row = jnp.where(lanes == r, squares, squares_row)
        duals_row = jnp.where(lanes == r, dual, duals_row)
        for copy in copies:
            copy.wait_send()
        return alpha, margins, weights, squares_row, duals_row, norms

    zero = jnp.zeros((1, held), F32)
    blank = jnp.zeros((1, 128), F32)
    alpha, _, weights, squares_row, duals_row, norms = lax.fori_loop(
        0,
        ROUNDS,
        one_round,
        (zero, zero, jnp.zeros((1, width), F32), blank, blank, blank),
    )

    copies = []
    stat_y[0, my] = jnp.concatenate([squares_row, duals_row], axis=0)
    for d in y_far_first:
        copies.append(
            send(
                stat_y.at[0, my],
                stat_y.at[0, my],
                out_stat_y.at[d],
                sem_stat_y.at[0, my],
                {"y": y_at(d)},
            )
        )
    dual_buf[0, my] = jnp.sum(dot_t(three_rows(alpha, 16), chosen[...]), axis=0, keepdims=True)
    for d in y_far_first:
        copies.append(
            send(
                dual_buf.at[0, my],
                dual_buf.at[0, my],
                out_dual.at[d],
                sem_dual.at[0, my],
                {"y": y_at(d)},
            )
        )
    weights_out[...] = weights
    for d in range(1, ny):
        received(stat_y, sem_stat_y, out_stat_y, 0, y_at(d), {"y": y_at(d)})
    stats = added(stat_y, 0, ny)
    if nx > 1:
        stat_x[0, mx] = stats
        copies += exchange(stat_x, sem_stat_x, out_stat_x, 0, mx, nx, "x")
        stats = added(stat_x, 0, nx)
    for d in range(1, ny):
        received(dual_buf, sem_dual, out_dual, 0, y_at(d), {"y": y_at(d)})
    duals_out[...] = added(dual_buf, 0, ny)
    if nz > 1:
        stat_z[0, mz] = stats
        copies += exchange(stat_z, sem_stat_z, out_stat_z, 0, mz, nz, "z")
        stats = added(stat_z, 0, nz)
    primal = stats[0:1, :] / (2.0 * total_samples) + 0.5 * ridge * norms
    dual = stats[1:2, :] / total_samples - 0.5 * ridge * norms
    objectives_out[0:1, :] = primal[:, 0:ROUNDS]
    objectives_out[1:2, :] = dual[:, 0:ROUNDS]
    for copy in started + copies:
        copy.wait_send()


def on_device(sizes, inputs, frequencies, phases, targets, block_order):
    nx, nz, ny, nc = sizes
    rows, raw = inputs.shape
    width = frequencies.shape[1]
    held = nc * BLOCK
    vmem = pl.BlockSpec(memory_space=pltpu.VMEM)
    dma = pltpu.SemaphoreType.DMA
    scratch = [
        pltpu.VMEM((held, 128), BF16),
        pltpu.VMEM((rows, held), BF16),
        pltpu.VMEM((ny, 128, width), BF16),
        pltpu.VMEM((ny, 1, width), F32),
        pltpu.VMEM((held, ny * width), BF16),
        pltpu.VMEM((nc, BLOCK, BLOCK), F32),
        pltpu.VMEM((BLOCK, BLOCK), F32),
        pltpu.VMEM((2 * BLOCK, BLOCK), F32),
        pltpu.VMEM((nc, BLOCK, BLOCK), F32),
        pltpu.VMEM((held, 128), F32),
        pltpu.VMEM((held, 128), F32),
        pltpu.VMEM((ROUNDS, ny, 1, width), F32),
        pltpu.VMEM((ROUNDS, ny, 1, width), F32),
        pltpu.VMEM((ROUNDS, nx, 1, width), F32),
        pltpu.VMEM((ROUNDS, nz, 1, width), F32),
        pltpu.VMEM((ROUNDS, ny, 1, width), F32),
        pltpu.VMEM((ROUNDS, nc, 1, held + 128), F32),
        pltpu.VMEM((1, ny, 1, rows), F32),
        pltpu.VMEM((1, ny, 2, 128), F32),
        pltpu.VMEM((1, nx, 2, 128), F32),
        pltpu.VMEM((1, nz, 2, 128), F32),
        dma((ny, PIECES)),
        dma((ny,)),
        dma((1,)),
        dma((nc,)),
        dma((ROUNDS, ny)),
        dma((ROUNDS, nx)),
        dma((ROUNDS, nz)),
        dma((ROUNDS, ny)),
        dma((ROUNDS, nc)),
        dma((1, ny)),
        dma((1, ny)),
        dma((1, nx)),
        dma((1, nz)),
        dma((PIECES,)),
        dma((PIECES,)),
        dma((PIECES,)),
        dma((ny,)),
        dma((2,)),
        dma((ny,)),
        dma((nx,)),
        dma((nz,)),
        dma((ny,)),
        dma((1,)),
        dma((ny,)),
        dma((ny,)),
        dma((nx,)),
        dma((nz,)),
    ]
    weights, duals, objectives = pl.pallas_call(
        functools.partial(kernel, sizes),
        out_shape=(
            jax.ShapeDtypeStruct((1, width), F32),
            jax.ShapeDtypeStruct((1, rows), F32),
            jax.ShapeDtypeStruct((2, ROUNDS), F32),
        ),
        in_specs=[vmem] * 5,
        out_specs=(vmem, vmem, vmem),
        scratch_shapes=scratch,
        compiler_params=pltpu.CompilerParams(
            collective_id=0, has_side_effects=True, vmem_limit_bytes=60 * 1024 * 1024
        ),
        name="cocoa",
    )(
        inputs.T,
        frequencies,
        phases.reshape(1, width),
        targets.reshape(1, rows),
        block_order.reshape(1, rows),
    )
    return weights.reshape(width), duals.reshape(rows), objectives.T


def solution(mesh):
    devices = mesh.devices
    samp, feat = mesh.shape["samp"], mesh.shape["feat"]
    nc = 2
    ny = feat // nc
    nx = 4 if samp == 32 else 1
    nz = samp // nx
    torus = Mesh(devices.reshape(nx, nz, ny, nc), ("x", "z", "y", "core"))
    samp_axes, feat_axes = ("x", "z"), ("y", "core")
    in_specs = (
        P(samp_axes, None),
        P(None, feat_axes),
        P(feat_axes),
        P(samp_axes),
        P(samp_axes),
    )
    out_specs = (P(feat_axes), P(samp_axes), P())
    return jax.shard_map(
        functools.partial(on_device, (nx, nz, ny, nc)),
        mesh=torus,
        in_specs=in_specs,
        out_specs=out_specs,
        check_vma=False,
    )
```

time: 139 us -> 129 us (0.928)
  Pallas kernels: 134 us -> 125 us
  local copies, waits for them, and re-layouts: 4.62 us -> 2.62 us
    pallas_call x1, Pallas kernels: 134 us -> 125 us  [on_device(): pl.pallas_call(functools.partial(kernel, sizes), out_shape=(jax.ShapeDtyp...]
    unnamed x8 -> x9, local copies, waits for them, and re-layouts: 4.62 us -> 2.62 us
where the time goes in v2:
time: 129 us
  Pallas kernels  125 us (97%)
  local copies, waits for them, and re-layouts  2.62 us (2%)
    pallas_call x1, Pallas kernels, on_device(): pl.pallas_call(functools.partial(kernel, sizes), out_shape=(jax.ShapeDtyp...  125 us
    unnamed x9, local copies, waits for them, and re-layouts  2.62 us

profile of v2, /device:TPU:8, one launch (start us, length us, event | category | flops | bytes accessed | tf_op | source)
XLA Modules:
  0.0 128.6 jit_solution(13231578154116955025)
XLA Ops:
  0.6 125.4 %cocoa.1 = (f32[1,2048]{1,0:T(1,128)}, f32[1,2048]{1,0:T(1,128)}, f32[2,4]{1,0:T(2,128)}) custom-call(bf16[96,2048]{1,0:T(8,128)(2,1)} %bitcast.7, bf16[96,2048]{1,0:T(8,128)(2,1)} %freq_ref.1, f32[1,2048]{1,0:T(1,128)} %bitcast.8, f32[1,2048]{1,0:T(1,128)} %bitcast.9, s32[1,2048]{1,0:T(1,128)} %bitcast.10), custom_call_target="tpu_custom_call" | custom-call | tf_op jit(solution)/shard_map/cocoa/pallas_call | solution.py:570
  126.0 0.0 copy-start.1
  126.0 0.7 copy-done.1
  126.7 0.0 copy-start
  126.7 0.6 copy.11
  127.3 0.1 copy-done
  127.4 0.0 copy-start.2
  127.4 0.6 copy.12
  128.0 0.1 copy-done.2
  128.1 0.6 copy.13
Async XLA Ops:
  126.0 0.7 copy-start.1
  126.7 0.7 copy-start
  127.4 0.7 copy-start.2

commit v3 on v2

--- a/solution.py
+++ b/solution.py
@@ -80,26 +80,22 @@
     margin_c,
     rs_send,
     rs_recv,
-    x_buf,
     z_buf,
     ag_buf,
     margin_buf,
     dual_buf,
-    stat_y,
-    stat_x,
+    stat_g,
     stat_z,
     sem_piece,
     sem_phase,
     sem_gram,
     sem_inverse,
     sem_rs,
-    sem_x,
     sem_z,
     sem_ag,
     sem_margin,
     sem_dual,
-    sem_stat_y,
-    sem_stat_x,
+    sem_stat_g,
     sem_stat_z,
     out_right,
     out_left,
@@ -107,13 +103,11 @@
     out_phase,
     out_swap,
     out_rs,
-    out_x,
     out_z,
     out_ag,
     out_margin,
     out_dual,
-    out_stat_y,
-    out_stat_x,
+    out_stat_g,
     out_stat_z,
 ):
     nx, nz, ny, nc = sizes
@@ -122,6 +116,8 @@
     total_features = width * ny * nc
     total_samples = rows * nx * nz
     held = nc * BLOCK
+    members = ny * nx
+    share = width // nx
     piece = width // PIECES
     half = PIECES // 2
     step_scale = BLOCK / total_samples
@@ -136,9 +132,21 @@
 
     y_far_first = sorted(range(1, ny), key=lambda d: (-min(d, ny - d), d))
 
+    def hops(d, n):
+        return min(d, n - d)
+
+    others = sorted(
+        [(dy, dx) for dy in range(ny) for dx in range(nx) if (dy, dx) != (0, 0)],
+        key=lambda o: (-hops(o[0], ny) - hops(o[1], nx), o),
+    )
+    mine = my * nx + mx
+
+    def member(dy, dx):
+        y, x = lax.rem(my + dy, ny), lax.rem(mx + dx, nx)
+        return {"y": y, "x": x}, y * nx + x
+
     barrier = pltpu.get_barrier_semaphore()
-    peers = [partner] + [{"y": y_at(d)} for d in y_far_first]
-    peers += [{"x": lax.rem(mx + d, nx)} for d in range(1, nx)]
+    peers = [partner] + [member(dy, dx)[0] for dy, dx in others]
     peers += [{"z": lax.rem(mz + d, nz)} for d in range(1, nz)]
     for peer in peers:
         pl.semaphore_signal(barrier, inc=1, device_id=peer, device_id_type=MESH)
@@ -331,12 +339,15 @@
             value = value + buf[at, k]
         return value
 
-    group = min(512, width)
-
-    def weigh(shard):
+    def share_at(index, g, size):
+        return pl.ds(pl.multiple_of(index * share + g * size, size), size)
+
+    group = min(512, share)
+
+    def weigh(index):
         done = []
-        for g in range(width // group):
-            at = pl.ds(pl.multiple_of(shard * width + g * group, group), group)
+        for g in range(share // group):
+            at = share_at(index, g, group)
             total = jnp.zeros((16, group), F32)
             for t in range(held // 16):
                 by = delta_c[t * 16 : (t + 1) * 16, :]
@@ -345,20 +356,28 @@
             done.append(jnp.sum(total, axis=0, keepdims=True))
         return jnp.concatenate(done, axis=1) * step_scale
 
-    def add_margins(shard, weight):
+    def add_margins(index, weight, first=False):
         used = weight.astype(BF16).astype(F32)
         tall = 64
-
-        def some_rows(t, _):
-            at = pl.ds(pl.multiple_of(t * tall, tall), tall)
-            total = margin_c[at, :]
-            for g in range(width // 128):
-                columns = pl.ds(pl.multiple_of(shard * width + g * 128, 128), 128)
+        for t in range(held // tall):
+            at = slice(t * tall, (t + 1) * tall)
+            total = jnp.zeros((tall, 128), F32) if first else margin_c[at, :]
+            for g in range(share // 128):
+                columns = share_at(index, g, 128)
                 total = total + phi[at, columns].astype(F32) * used[:, g * 128 : (g + 1) * 128]
             margin_c[at, :] = total
-            return 0
-
-        lax.fori_loop(0, held // tall, some_rows, 0)
+
+    def to_members(src, dst, out_sems, sem, at):
+        copies = []
+        for k, (dy, dx) in enumerate(others):
+            device, _ = member(dy, dx)
+            copies.append(send(src.at[at, mine], dst.at[at, mine], out_sems.at[k], sem.at[at, mine], device))
+        return copies
+
+    def from_member(buf, sem_in, sem_out, at, dy, dx):
+        device, index = member(dy, dx)
+        received(buf, sem_in, sem_out, at, index, device)
+        return index
 
     def one_round(r, carry):
         alpha, margins, weights, squares_row, duals_row, norms = carry
@@ -370,18 +389,13 @@
         column = jnp.broadcast_to(jnp.concatenate(parts, axis=0), (held, 128))
         delta_c[...] = column.astype(BF16).astype(F32)
         copies = []
-        for d in y_far_first:
-            rs_send[r, d] = weigh(y_at(d))
+        for k, (dy, dx) in enumerate(others):
+            device, index = member(dy, dx)
+            rs_send[r, k] = weigh(index)
             copies.append(
-                send(
-                    rs_send.at[r, d],
-                    rs_recv.at[r, my],
-                    out_rs.at[d],
-                    sem_rs.at[r, my],
-                    {"y": y_at(d)},
-                )
+                send(rs_send.at[r, k], rs_recv.at[r, mine], out_rs.at[k], sem_rs.at[r, mine], device)
             )
-        rs_recv[r, my] = weigh(my)
+        rs_recv[r, mine] = weigh(mine)
         turned = jnp.concatenate(
             [
                 jnp.transpose(column[t * 128 : (t + 1) * 128, :])[0:1, :]
@@ -390,34 +404,20 @@
             axis=1,
         )
         alpha = alpha + turned
-        for d in range(1, ny):
-            received(rs_recv, sem_rs, out_rs, r, y_at(d), {"y": y_at(d)})
-        part = added(rs_recv, r, ny)
-        if nx > 1:
-            x_buf[r, mx] = part
-            copies += exchange(x_buf, sem_x, out_x, r, mx, nx, "x")
-            part = added(x_buf, r, nx)
+        for dy, dx in reversed(others):
+            from_member(rs_recv, sem_rs, out_rs, r, dy, dx)
+        part = added(rs_recv, r, members)
         if nz > 1:
             z_buf[r, mz] = part
             copies += exchange(z_buf, sem_z, out_z, r, mz, nz, "z")
             part = added(z_buf, r, nz)
         weights = weights + part
-        ag_buf[r, my] = weights
-        for d in y_far_first:
-            copies.append(
-                send(
-                    ag_buf.at[r, my],
-                    ag_buf.at[r, my],
-                    out_ag.at[d],
-                    sem_ag.at[r, my],
-                    {"y": y_at(d)},
-                )
-            )
-        margin_c[...] = jnp.zeros_like(margin_c)
-        add_margins(my, weights)
-        for d in reversed(y_far_first):
-            received(ag_buf, sem_ag, out_ag, r, y_at(d), {"y": y_at(d)})
-            add_margins(y_at(d), ag_buf[r, y_at(d)])
+        ag_buf[r, mine] = weights
+        copies += to_members(ag_buf, ag_buf, out_ag, sem_ag, r)
+        add_margins(mine, weights, first=True)
+        for dy, dx in reversed(others):
+            index = from_member(ag_buf, sem_ag, out_ag, r, dy, dx)
+            add_margins(index, ag_buf[r, index])
         row = jnp.concatenate(
             [
                 jnp.sum(
@@ -428,7 +428,7 @@
             axis=1,
         )
         whole = ag_buf[r, 0] * ag_buf[r, 0]
-        for k in range(1, ny):
+        for k in range(1, members):
             whole = whole + ag_buf[r, k] * ag_buf[r, k]
         norm = jnp.sum(whole, axis=1, keepdims=True)
         margin_buf[r, mc, :, 0:held] = row
@@ -457,25 +457,15 @@
 
     zero = jnp.zeros((1, held), F32)
     blank = jnp.zeros((1, 128), F32)
-    alpha, _, weights, squares_row, duals_row, norms = lax.fori_loop(
+    alpha, _, _, squares_row, duals_row, norms = lax.fori_loop(
         0,
         ROUNDS,
         one_round,
-        (zero, zero, jnp.zeros((1, width), F32), blank, blank, blank),
-    )
-
-    copies = []
-    stat_y[0, my] = jnp.concatenate([squares_row, duals_row], axis=0)
-    for d in y_far_first:
-        copies.append(
-            send(
-                stat_y.at[0, my],
-                stat_y.at[0, my],
-                out_stat_y.at[d],
-                sem_stat_y.at[0, my],
-                {"y": y_at(d)},
-            )
-        )
+        (zero, zero, jnp.zeros((1, share), F32), blank, blank, blank),
+    )
+
+    stat_g[0, mine] = jnp.concatenate([squares_row, duals_row], axis=0)
+    copies = to_members(stat_g, stat_g, out_stat_g, sem_stat_g, 0)
     dual_buf[0, my] = jnp.sum(dot_t(three_rows(alpha, 16), chosen[...]), axis=0, keepdims=True)
     for d in y_far_first:
         copies.append(
@@ -487,21 +477,19 @@
                 {"y": y_at(d)},
             )
         )
-    weights_out[...] = weights
-    for d in range(1, ny):
-        received(stat_y, sem_stat_y, out_stat_y, 0, y_at(d), {"y": y_at(d)})
-    stats = added(stat_y, 0, ny)
-    if nx > 1:
-        stat_x[0, mx] = stats
-        copies += exchange(stat_x, sem_stat_x, out_stat_x, 0, mx, nx, "x")
-        stats = added(stat_x, 0, nx)
-    for d in range(1, ny):
-        received(dual_buf, sem_dual, out_dual, 0, y_at(d), {"y": y_at(d)})
-    duals_out[...] = added(dual_buf, 0, ny)
+    weights_out[...] = jnp.concatenate(
+        [ag_buf[ROUNDS - 1, my * nx + k] for k in range(nx)], axis=1
+    )
+    for dy, dx in reversed(others):
+        from_member(stat_g, sem_stat_g, out_stat_g, 0, dy, dx)
+    stats = added(stat_g, 0, members)
     if nz > 1:
         stat_z[0, mz] = stats
         copies += exchange(stat_z, sem_stat_z, out_stat_z, 0, mz, nz, "z")
         stats = added(stat_z, 0, nz)
+    for d in range(1, ny):
+        received(dual_buf, sem_dual, out_dual, 0, y_at(d), {"y": y_at(d)})
+    duals_out[...] = added(dual_buf, 0, ny)
     primal = stats[0:1, :] / (2.0 * total_samples) + 0.5 * ridge * norms
     dual = stats[1:2, :] / total_samples - 0.5 * ridge * norms
     objectives_out[0:1, :] = primal[:, 0:ROUNDS]
@@ -515,6 +503,8 @@
     rows, raw = inputs.shape
     width = frequencies.shape[1]
     held = nc * BLOCK
+    members = ny * nx
+    share = width // nx
     vmem = pl.BlockSpec(memory_space=pltpu.VMEM)
     dma = pltpu.SemaphoreType.DMA
     scratch = [
@@ -529,42 +519,36 @@
         pltpu.VMEM((nc, BLOCK, BLOCK), F32),
         pltpu.VMEM((held, 128), F32),
         pltpu.VMEM((held, 128), F32),
-        pltpu.VMEM((ROUNDS, ny, 1, width), F32),
-        pltpu.VMEM((ROUNDS, ny, 1, width), F32),
-        pltpu.VMEM((ROUNDS, nx, 1, width), F32),
-        pltpu.VMEM((ROUNDS, nz, 1, width), F32),
-        pltpu.VMEM((ROUNDS, ny, 1, width), F32),
+        pltpu.VMEM((ROUNDS, members, 1, share), F32),
+        pltpu.VMEM((ROUNDS, members, 1, share), F32),
+        pltpu.VMEM((ROUNDS, nz, 1, share), F32),
+        pltpu.VMEM((ROUNDS, members, 1, share), F32),
         pltpu.VMEM((ROUNDS, nc, 1, held + 128), F32),
         pltpu.VMEM((1, ny, 1, rows), F32),
-        pltpu.VMEM((1, ny, 2, 128), F32),
-        pltpu.VMEM((1, nx, 2, 128), F32),
+        pltpu.VMEM((1, members, 2, 128), F32),
         pltpu.VMEM((1, nz, 2, 128), F32),
         dma((ny, PIECES)),
         dma((ny,)),
         dma((1,)),
         dma((nc,)),
-        dma((ROUNDS, ny)),
-        dma((ROUNDS, nx)),
+        dma((ROUNDS, members)),
         dma((ROUNDS, nz)),
-        dma((ROUNDS, ny)),
+        dma((ROUNDS, members)),
         dma((ROUNDS, nc)),
         dma((1, ny)),
-        dma((1, ny)),
-        dma((1, nx)),
+        dma((1, members)),
         dma((1, nz)),
         dma((PIECES,)),
         dma((PIECES,)),
         dma((PIECES,)),
         dma((ny,)),
         dma((2,)),
-        dma((ny,)),
-        dma((nx,)),
+        dma((members,)),
         dma((nz,)),
-        dma((ny,)),
+        dma((members,)),
         dma((1,)),
         dma((ny,)),
-        dma((ny,)),
-        dma((nx,)),
+        dma((members,)),
         dma((nz,)),
     ]
     weights, duals, objectives = pl.pallas_call(
@@ -596,7 +580,7 @@
     samp, feat = mesh.shape["samp"], mesh.shape["feat"]
     nc = 2
     ny = feat // nc
-    nx = 4 if samp == 32 else 1
+    nx = math.gcd(samp, 4)
     nz = samp // nx
     torus = Mesh(devices.reshape(nx, nz, ny, nc), ("x", "z", "y", "core"))
     samp_axes, feat_axes = ("x", "z"), ("y", "core")

time: 129 us -> 120 us (0.930)
  Pallas kernels: 125 us -> 116 us
    pallas_call x1, Pallas kernels: 125 us -> 116 us  [on_device(): pl.pallas_call(functools.partial(kernel, sizes), out_shape=(jax.ShapeDtyp...]
where the time goes in v3:
time: 120 us; the launch traced here: 119 us
  Pallas kernels  116 us (97%)
  local copies, waits for them, and re-layouts  2.62 us (2%)
    pallas_call x1, Pallas kernels, on_device(): pl.pallas_call(functools.partial(kernel, sizes), out_shape=(jax.ShapeDtyp...  116 us
    unnamed x9, local copies, waits for them, and re-layouts  2.62 us

profile of v3, /device:TPU:8, one launch (start us, length us, event | category | flops | bytes accessed | tf_op | source)
XLA Modules:
  0.0 118.8 jit_solution(14038661000974768801)
XLA Ops:
  0.6 115.6 %cocoa.1 = (f32[1,2048]{1,0:T(1,128)}, f32[1,2048]{1,0:T(1,128)}, f32[2,4]{1,0:T(2,128)}) custom-call(bf16[96,2048]{1,0:T(8,128)(2,1)} %bitcast.7, bf16[96,2048]{1,0:T(8,128)(2,1)} %freq_ref.1, f32[1,2048]{1,0:T(1,128)} %bitcast.8, f32[1,2048]{1,0:T(1,128)} %bitcast.9, s32[1,2048]{1,0:T(1,128)} %bitcast.10), custom_call_target="tpu_custom_call" | custom-call | tf_op jit(solution)/shard_map/cocoa/pallas_call | solution.py:554
  116.2 0.0 copy-start.1
  116.2 0.7 copy-done.1
  116.9 0.0 copy-start
  116.9 0.6 copy.11
  117.5 0.1 copy-done
  117.6 0.0 copy-start.2
  117.6 0.6 copy.12
  118.2 0.1 copy-done.2
  118.3 0.6 copy.13
Async XLA Ops:
  116.2 0.7 copy-start.1
  116.9 0.7 copy-start
  117.6 0.7 copy-start.2

commit v4 on v3

--- a/solution.py
+++ b/solution.py
@@ -59,14 +59,17 @@
 
 def kernel(
     sizes,
-    inputs_ref,
-    freq_ref,
-    phase_ref,
-    target_ref,
-    order_ref,
+    inputs_hbm,
+    freq_hbm,
+    phase_hbm,
+    target_hbm,
+    order_hbm,
     weights_out,
     duals_out,
     objectives_out,
+    inputs_ref,
+    target_ref,
+    order_ref,
     picked_b,
     chosen,
     freq,
@@ -78,14 +81,18 @@
     inverse,
     delta_c,
     margin_c,
+    margin_rows,
+    alpha_rows,
     rs_send,
     rs_recv,
     z_buf,
     ag_buf,
     margin_buf,
+    norm_buf,
     dual_buf,
     stat_g,
     stat_z,
+    sem_in,
     sem_piece,
     sem_phase,
     sem_gram,
@@ -94,6 +101,7 @@
     sem_z,
     sem_ag,
     sem_margin,
+    sem_norm,
     sem_dual,
     sem_stat_g,
     sem_stat_z,
@@ -111,8 +119,8 @@
     out_stat_z,
 ):
     nx, nz, ny, nc = sizes
-    raw, rows = inputs_ref.shape
-    width = freq_ref.shape[1]
+    raw, rows = inputs_hbm.shape
+    width = freq_hbm.shape[1]
     total_features = width * ny * nc
     total_samples = rows * nx * nz
     held = nc * BLOCK
@@ -150,6 +158,21 @@
     peers += [{"z": lax.rem(mz + d, nz)} for d in range(1, nz)]
     for peer in peers:
         pl.semaphore_signal(barrier, inc=1, device_id=peer, device_id_type=MESH)
+    loads = [
+        pltpu.make_async_copy(src, dst, sem_in.at[k])
+        for k, (src, dst) in enumerate(
+            [
+                (order_hbm, order_ref),
+                (inputs_hbm, inputs_ref),
+                (freq_hbm, freq.at[my, pl.ds(0, raw), :]),
+                (phase_hbm, phases.at[my]),
+                (target_hbm, target_ref),
+            ]
+        )
+    ]
+    for load in loads:
+        load.start()
+    loads[0].wait()
 
     own_order = order_ref[:, pl.ds(pl.multiple_of(my * held, held), held)]
     for part in range(rows // BLOCK):
@@ -159,9 +182,12 @@
         ).astype(BF16)
     line = lax.broadcasted_iota(jnp.int32, (128 - raw, held), 0)
     ones = jnp.where(line < 3, 1.0, 0.0)
+    loads[1].wait()
     picked = jnp.concatenate([dot(inputs_ref[...], chosen[...]), ones], axis=0)
     picked_b[...] = jnp.transpose(picked).astype(BF16)
 
+    for load in loads[2:]:
+        load.wait()
     pl.semaphore_wait(barrier, len(peers))
 
     def remote(src, dst, out_sem, in_sem, device):
@@ -189,21 +215,19 @@
     started = []
     for d in y_far_first:
         started.append(
-            send(phase_ref, phases.at[my], out_phase.at[d], sem_phase.at[my], {"y": y_at(d)})
+            send(phases.at[my], phases.at[my], out_phase.at[d], sem_phase.at[my], {"y": y_at(d)})
         )
     for i in range(PIECES):
         for q, out, y in ((i, out_right, y_right), ((i + half) % PIECES, out_left, y_left)):
             started.append(
                 send(
-                    freq_ref.at[:, pl.ds(q * piece, piece)],
+                    freq_piece(my, q),
                     freq_piece(my, q),
                     out.at[q],
                     sem_piece.at[my, q],
                     {"y": y},
                 )
             )
-    freq[my, 0:raw, :] = freq_ref[...]
-    phases[my] = phase_ref[...]
     wanted = jnp.sum(dot(three_rows(target_ref[...], 16), chosen[...]), axis=0, keepdims=True)
 
     amplitude = math.sqrt(2.0 / total_features)
@@ -242,7 +266,7 @@
 
     def phases_in(shard):
         remote(
-            phase_ref, phases.at[shard], out_phase.at[0], sem_phase.at[shard], {"y": y_left}
+            phases.at[shard], phases.at[shard], out_phase.at[0], sem_phase.at[shard], {"y": y_left}
         ).wait_recv()
 
     def relay(shard, q, y):
@@ -380,7 +404,7 @@
         return index
 
     def one_round(r, carry):
-        alpha, margins, weights, squares_row, duals_row, norms = carry
+        alpha, margins, weights = carry
         rest = wanted - alpha - margins
         parts = []
         for b in range(nc):
@@ -427,12 +451,7 @@
             ],
             axis=1,
         )
-        whole = ag_buf[r, 0] * ag_buf[r, 0]
-        for k in range(1, members):
-            whole = whole + ag_buf[r, k] * ag_buf[r, k]
-        norm = jnp.sum(whole, axis=1, keepdims=True)
-        margin_buf[r, mc, :, 0:held] = row
-        margin_buf[r, mc, :, held:] = jnp.broadcast_to(norm, (1, 128))
+        margin_buf[r, mc] = row
         copies.append(
             send(
                 margin_buf.at[r, mc],
@@ -443,29 +462,43 @@
             )
         )
         received(margin_buf, sem_margin, out_margin, r, other, partner)
-        both = added(margin_buf, r, nc)
-        margins = both[:, 0:held]
-        norms = jnp.where(lanes == r, both[:, held:], norms)
-        off = margins - wanted
-        squares = jnp.sum(off * off, axis=1, keepdims=True)
-        dual = jnp.sum(alpha * wanted - 0.5 * alpha * alpha, axis=1, keepdims=True)
-        squares_row = jnp.where(lanes == r, squares, squares_row)
-        duals_row = jnp.where(lanes == r, dual, duals_row)
+        margins = added(margin_buf, r, nc)
+        margin_rows[r] = margins
+        alpha_rows[r] = alpha
         for copy in copies:
             copy.wait_send()
-        return alpha, margins, weights, squares_row, duals_row, norms
+        return alpha, margins, weights
 
     zero = jnp.zeros((1, held), F32)
-    blank = jnp.zeros((1, 128), F32)
-    alpha, _, _, squares_row, duals_row, norms = lax.fori_loop(
+    alpha, _, _ = lax.fori_loop(
         0,
         ROUNDS,
         one_round,
-        (zero, zero, jnp.zeros((1, share), F32), blank, blank, blank),
-    )
-
-    stat_g[0, mine] = jnp.concatenate([squares_row, duals_row], axis=0)
+        (zero, zero, jnp.zeros((1, share), F32)),
+    )
+
+    def in_lanes(values):
+        line = jnp.zeros((1, 128), F32)
+        for r, value in enumerate(values):
+            line = jnp.where(lanes == r, jnp.sum(value, axis=1, keepdims=True), line)
+        return line
+
+    squares = in_lanes([(margin_rows[r] - wanted) ** 2 for r in range(ROUNDS)])
+    gains = in_lanes(
+        [alpha_rows[r] * wanted - 0.5 * alpha_rows[r] * alpha_rows[r] for r in range(ROUNDS)]
+    )
+    stat_g[0, mine] = jnp.concatenate([squares, gains], axis=0)
     copies = to_members(stat_g, stat_g, out_stat_g, sem_stat_g, 0)
+    wholes = []
+    for r in range(ROUNDS):
+        whole = ag_buf[r, 0] * ag_buf[r, 0]
+        for k in range(1, members):
+            whole = whole + ag_buf[r, k] * ag_buf[r, k]
+        wholes.append(whole)
+    norm_buf[0, mc] = in_lanes(wholes)
+    copies.append(
+        send(norm_buf.at[0, mc], norm_buf.at[0, mc], out_swap.at[2], sem_norm.at[0, mc], partner)
+    )
     dual_buf[0, my] = jnp.sum(dot_t(three_rows(alpha, 16), chosen[...]), axis=0, keepdims=True)
     for d in y_far_first:
         copies.append(
@@ -490,12 +523,20 @@
     for d in range(1, ny):
         received(dual_buf, sem_dual, out_dual, 0, y_at(d), {"y": y_at(d)})
     duals_out[...] = added(dual_buf, 0, ny)
+    received(norm_buf, sem_norm, out_swap, 0, other, partner)
+    norms = added(norm_buf, 0, nc)
     primal = stats[0:1, :] / (2.0 * total_samples) + 0.5 * ridge * norms
     dual = stats[1:2, :] / total_samples - 0.5 * ridge * norms
     objectives_out[0:1, :] = primal[:, 0:ROUNDS]
     objectives_out[1:2, :] = dual[:, 0:ROUNDS]
     for copy in started + copies:
         copy.wait_send()
+
+
+def copied(weights, duals, objectives, weights_out, duals_out, objectives_out):
+    weights_out[...] = weights[...]
+    duals_out[...] = duals[...]
+    objectives_out[...] = objectives[...]
 
 
 def on_device(sizes, inputs, frequencies, phases, targets, block_order):
@@ -508,6 +549,9 @@
     vmem = pl.BlockSpec(memory_space=pltpu.VMEM)
     dma = pltpu.SemaphoreType.DMA
     scratch = [
+        pltpu.VMEM((raw, rows), BF16),
+        pltpu.VMEM((1, rows), F32),
+        pltpu.VMEM((1, rows), jnp.int32),
         pltpu.VMEM((held, 128), BF16),
         pltpu.VMEM((rows, held), BF16),
         pltpu.VMEM((ny, 128, width), BF16),
@@ -519,14 +563,18 @@
         pltpu.VMEM((nc, BLOCK, BLOCK), F32),
         pltpu.VMEM((held, 128), F32),
         pltpu.VMEM((held, 128), F32),
+        pltpu.VMEM((ROUNDS, 1, held), F32),
+        pltpu.VMEM((ROUNDS, 1, held), F32),
         pltpu.VMEM((ROUNDS, members, 1, share), F32),
         pltpu.VMEM((ROUNDS, members, 1, share), F32),
         pltpu.VMEM((ROUNDS, nz, 1, share), F32),
         pltpu.VMEM((ROUNDS, members, 1, share), F32),
-        pltpu.VMEM((ROUNDS, nc, 1, held + 128), F32),
+        pltpu.VMEM((ROUNDS, nc, 1, held), F32),
+        pltpu.VMEM((1, nc, 1, 128), F32),
         pltpu.VMEM((1, ny, 1, rows), F32),
         pltpu.VMEM((1, members, 2, 128), F32),
         pltpu.VMEM((1, nz, 2, 128), F32),
+        dma((5,)),
         dma((ny, PIECES)),
         dma((ny,)),
         dma((1,)),
@@ -535,6 +583,7 @@
         dma((ROUNDS, nz)),
         dma((ROUNDS, members)),
         dma((ROUNDS, nc)),
+        dma((1, nc)),
         dma((1, ny)),
         dma((1, members)),
         dma((1, nz)),
@@ -542,7 +591,7 @@
         dma((PIECES,)),
         dma((PIECES,)),
         dma((ny,)),
-        dma((2,)),
+        dma((3,)),
         dma((members,)),
         dma((nz,)),
         dma((members,)),
@@ -551,14 +600,15 @@
         dma((members,)),
         dma((nz,)),
     ]
-    weights, duals, objectives = pl.pallas_call(
+    shapes = (
+        jax.ShapeDtypeStruct((1, width), F32),
+        jax.ShapeDtypeStruct((1, rows), F32),
+        jax.ShapeDtypeStruct((2, ROUNDS), F32),
+    )
+    results = pl.pallas_call(
         functools.partial(kernel, sizes),
-        out_shape=(
-            jax.ShapeDtypeStruct((1, width), F32),
-            jax.ShapeDtypeStruct((1, rows), F32),
-            jax.ShapeDtypeStruct((2, ROUNDS), F32),
-        ),
-        in_specs=[vmem] * 5,
+        out_shape=shapes,
+        in_specs=[pl.BlockSpec(memory_space=pl.ANY)] * 5,
         out_specs=(vmem, vmem, vmem),
         scratch_shapes=scratch,
         compiler_params=pltpu.CompilerParams(
@@ -572,6 +622,13 @@
         targets.reshape(1, rows),
         block_order.reshape(1, rows),
     )
+    weights, duals, objectives = pl.pallas_call(
+        copied,
+        out_shape=shapes,
+        in_specs=[vmem] * 3,
+        out_specs=(vmem, vmem, vmem),
+        name="results",
+    )(*results)
     return weights.reshape(width), duals.reshape(rows), objectives.T
 
 

time: 120 us -> 117 us (0.975)
  local copies, waits for them, and re-layouts: 2.62 us -> 0 us
    unnamed x9 -> x0, local copies, waits for them, and re-layouts: 2.62 us -> none
    pallas_call x1 -> x2, Pallas kernels: 116 us -> 116 us  [the longest x1 114 us: on_device(): pl.pallas_call(functools.partial(kernel, sizes), out_shape=shapes, in_spe...]
where the time goes in v4:
time: 117 us; the launch traced here: 116 us
  Pallas kernels  116 us (99%)
    pallas_call x1, Pallas kernels, on_device(): pl.pallas_call(functools.partial(kernel, sizes), out_shape=shapes, in_spe...  114 us

profile of v4, /device:TPU:8, one launch (start us, length us, event | category | flops | bytes accessed | tf_op | source)
XLA Modules:
  0.0 116.5 jit_solution(13199412753924420600)
XLA Ops:
  0.6 114.5 %cocoa.1 = (f32[1,2048]{1,0:T(1,128)}, f32[1,2048]{1,0:T(1,128)}, f32[2,4]{1,0:T(2,128)}) custom-call(bf16[96,2048]{1,0:T(8,128)(2,1)} %bitcast.7, bf16[96,2048]{1,0:T(8,128)(2,1)} %freq_hbm.1, f32[1,2048]{1,0:T(1,128)} %bitcast.8, f32[1,2048]{1,0:T(1,128)} %bitcast.9, s32[1,2048]{1,0:T(1,128)} %bitcast.10), custom_call_target="tpu_custom_call" | custom-call | tf_op jit(solution)/shard_map/cocoa/pallas_call | solution.py:608
  115.1 1.3 %results.1 = (f32[1,2048]{1,0:T(1,128)}, f32[1,2048]{1,0:T(1,128)}, f32[2,4]{1,0:T(2,128)}) custom-call(f32[1,2048]{1,0:T(1,128)} %get-tuple-element.9.weights, f32[1,2048]{1,0:T(1,128)} %get-tuple-element.10.duals, f32[2,4]{1,0:T(2,128)} %get-tuple-element.11.objectives), custom_call_target="tpu_custom_call" | custom-call | tf_op jit(solution)/shard_map/results/pallas_call | solution.py:625

commit v5 on v4

--- a/solution.py
+++ b/solution.py
@@ -41,6 +41,17 @@
     return lax.dot_general(
         a, b, (((1,), (0,)), ((), ())), precision=precision, preferred_element_type=F32
     )
+
+
+def halves(value):
+    high = value.astype(BF16)
+    return high, (value - high.astype(F32)).astype(BF16)
+
+
+def dot_3(a, b):
+    a_high, a_low = halves(a)
+    b_high, b_low = halves(b)
+    return dot(a_high, b_high) + (dot(a_high, b_low) + dot(a_low, b_high))
 
 
 def dot_t(a, b):
@@ -307,13 +318,13 @@
     first = 2.0 / (1.0 + TOP_EIGENVALUE)
     error = eye - first * gram_in[...]
     pair[0:BLOCK, :] = (scales[0] * first) * (eye + error)
-    pair[BLOCK:, :] = (1.0 - scales[0]) * eye + scales[0] * dot(error, error, HIGHEST)
+    pair[BLOCK:, :] = (1.0 - scales[0]) * eye + scales[0] * dot_3(error, error)
 
     def newton(k, _):
         scale = jnp.float32(scales[1])
         for n in range(2, len(scales)):
             scale = jnp.where(k == n, jnp.float32(scales[n]), scale)
-        product = dot(pair[...], pair[BLOCK:, :], HIGHEST)
+        product = dot_3(pair[...], pair[BLOCK:, :])
         pair[0:BLOCK, :] = scale * (pair[0:BLOCK, :] + product[0:BLOCK, :])
         pair[BLOCK:, :] = (1.0 - scale) * eye + scale * product[BLOCK:, :]
         return 0
@@ -321,7 +332,7 @@
     lax.fori_loop(1, len(scales), newton, 0)
     guess = pair[0:BLOCK, :]
     residual = eye - dot(gram_in[...], guess, HIGHEST)
-    inverse[mc] = guess + dot(guess, residual, HIGHEST)
+    inverse[mc] = guess + dot_3(guess, residual)
     started.append(
         send(inverse.at[mc], inverse.at[mc], out_swap.at[1], sem_inverse.at[mc], partner)
     )

time: 117 us -> 116 us (level)
  Pallas kernels: 116 us -> 114 us
    pallas_call x1, Pallas kernels: 114 us -> 113 us  [on_device(): pl.pallas_call(functools.partial(kernel, sizes), out_shape=shapes, in_spe...]
where the time goes in v5:
time: 116 us; the launch traced here: 115 us
  Pallas kernels  114 us (98%)
    pallas_call x1, Pallas kernels, on_device(): pl.pallas_call(functools.partial(kernel, sizes), out_shape=shapes, in_spe...  113 us

profile of v5, /device:TPU:8, one launch (start us, length us, event | category | flops | bytes accessed | tf_op | source)
XLA Modules:
  0.0 114.8 jit_solution(11790765921116239964)
XLA Ops:
  0.6 112.8 %cocoa.1 = (f32[1,2048]{1,0:T(1,128)}, f32[1,2048]{1,0:T(1,128)}, f32[2,4]{1,0:T(2,128)}) custom-call(bf16[96,2048]{1,0:T(8,128)(2,1)} %bitcast.7, bf16[96,2048]{1,0:T(8,128)(2,1)} %freq_hbm.1, f32[1,2048]{1,0:T(1,128)} %bitcast.8, f32[1,2048]{1,0:T(1,128)} %bitcast.9, s32[1,2048]{1,0:T(1,128)} %bitcast.10), custom_call_target="tpu_custom_call" | custom-call | tf_op jit(solution)/shard_map/cocoa/pallas_call | solution.py:619
  113.5 1.3 %results.1 = (f32[1,2048]{1,0:T(1,128)}, f32[1,2048]{1,0:T(1,128)}, f32[2,4]{1,0:T(2,128)}) custom-call(f32[1,2048]{1,0:T(1,128)} %get-tuple-element.9.weights, f32[1,2048]{1,0:T(1,128)} %get-tuple-element.10.duals, f32[2,4]{1,0:T(2,128)} %get-tuple-element.11.objectives), custom_call_target="tpu_custom_call" | custom-call | tf_op jit(solution)/shard_map/results/pallas_call | solution.py:636

commit v6 on v5

--- a/solution.py
+++ b/solution.py
@@ -344,7 +344,8 @@
 
     def exchange(buf, sem_in, sem_out, at, mine, count, axis):
         copies = []
-        for d in range(1, count):
+        far_first = sorted(range(1, count), key=lambda d: -hops(d, count))
+        for d in far_first:
             copies.append(
                 send(
                     buf.at[at, mine],
@@ -354,7 +355,7 @@
                     {axis: lax.rem(mine + d, count)},
                 )
             )
-        for d in range(1, count):
+        for d in reversed(far_first):
             source = lax.rem(mine + d, count)
             received(buf, sem_in, sem_out, at, source, {axis: source})
         return copies

time: 116 us -> 115 us (level)
  no operation moved by 1% of the time
where the time goes in v6:
time: 115 us; the launch traced here: 114 us
  Pallas kernels  114 us (99%)
    pallas_call x1, Pallas kernels, on_device(): pl.pallas_call(functools.partial(kernel, sizes), out_shape=shapes, in_spe...  112 us

profile of v6, /device:TPU:8, one launch (start us, length us, event | category | flops | bytes accessed | tf_op | source)
XLA Modules:
  0.0 114.4 jit_solution(16199786118456785207)
XLA Ops:
  0.6 112.5 %cocoa.1 = (f32[1,2048]{1,0:T(1,128)}, f32[1,2048]{1,0:T(1,128)}, f32[2,4]{1,0:T(2,128)}) custom-call(bf16[96,2048]{1,0:T(8,128)(2,1)} %bitcast.7, bf16[96,2048]{1,0:T(8,128)(2,1)} %freq_hbm.1, f32[1,2048]{1,0:T(1,128)} %bitcast.8, f32[1,2048]{1,0:T(1,128)} %bitcast.9, s32[1,2048]{1,0:T(1,128)} %bitcast.10), custom_call_target="tpu_custom_call" | custom-call | tf_op jit(solution)/shard_map/cocoa/pallas_call | solution.py:620
  113.1 1.3 %results.1 = (f32[1,2048]{1,0:T(1,128)}, f32[1,2048]{1,0:T(1,128)}, f32[2,4]{1,0:T(2,128)}) custom-call(f32[1,2048]{1,0:T(1,128)} %get-tuple-element.9.weights, f32[1,2048]{1,0:T(1,128)} %get-tuple-element.10.duals, f32[2,4]{1,0:T(2,128)} %get-tuple-element.11.objectives), custom_call_target="tpu_custom_call" | custom-call | tf_op jit(solution)/shard_map/results/pallas_call | solution.py:637

commit v7 on v6

--- a/solution.py
+++ b/solution.py
@@ -239,7 +239,6 @@
                     {"y": y},
                 )
             )
-    wanted = jnp.sum(dot(three_rows(target_ref[...], 16), chosen[...]), axis=0, keepdims=True)
 
     amplitude = math.sqrt(2.0 / total_features)
     coefs = [-amplitude * v for v in SINE]
@@ -309,6 +308,7 @@
             make_piece(y_far, q)
 
     swap = send(gram.at[other], gram_in, out_swap.at[0], sem_gram.at[0], partner)
+    wanted = jnp.sum(dot(three_rows(target_ref[...], 16), chosen[...]), axis=0, keepdims=True)
     row = lax.broadcasted_iota(jnp.int32, (BLOCK, BLOCK), 0)
     eye = jnp.where(row == lax.broadcasted_iota(jnp.int32, (BLOCK, BLOCK), 1), 1.0, 0.0)
     swap.wait()

time: 115 us -> 115 us (level)
  no operation moved by 1% of the time
where the time goes in v7:
time: 115 us; the launch traced here: 114 us
  Pallas kernels  114 us (99%)
    pallas_call x1, Pallas kernels, on_device(): pl.pallas_call(functools.partial(kernel, sizes), out_shape=shapes, in_spe...  112 us

profile of v7, /device:TPU:8, one launch (start us, length us, event | category | flops | bytes accessed | tf_op | source)
XLA Modules:
  0.0 114.4 jit_solution(3257094651830952584)
XLA Ops:
  0.6 112.5 %cocoa.1 = (f32[1,2048]{1,0:T(1,128)}, f32[1,2048]{1,0:T(1,128)}, f32[2,4]{1,0:T(2,128)}) custom-call(bf16[96,2048]{1,0:T(8,128)(2,1)} %bitcast.7, bf16[96,2048]{1,0:T(8,128)(2,1)} %freq_hbm.1, f32[1,2048]{1,0:T(1,128)} %bitcast.8, f32[1,2048]{1,0:T(1,128)} %bitcast.9, s32[1,2048]{1,0:T(1,128)} %bitcast.10), custom_call_target="tpu_custom_call" | custom-call | tf_op jit(solution)/shard_map/cocoa/pallas_call | solution.py:620
  113.1 1.3 %results.1 = (f32[1,2048]{1,0:T(1,128)}, f32[1,2048]{1,0:T(1,128)}, f32[2,4]{1,0:T(2,128)}) custom-call(f32[1,2048]{1,0:T(1,128)} %get-tuple-element.9.weights, f32[1,2048]{1,0:T(1,128)} %get-tuple-element.10.duals, f32[2,4]{1,0:T(2,128)} %get-tuple-element.11.objectives), custom_call_target="tpu_custom_call" | custom-call | tf_op jit(solution)/shard_map/results/pallas_call | solution.py:637
